TPU v7x, 32 devices: a whole 2x2x4 slice. The times are simulated.
32 devices in a mesh: dp: 4 (over x, core), expert: 8 (over z, y).
Axes of the slice: x: 2, y: 2, z: 4, core: 2. Of those that a mesh axis runs over, the one named last changes fastest.
Arguments:
- tokens: bfloat16 [32, 1024, 768], P('dp', 'expert'), may hold values from -6 to 6
- cotangent: bfloat16 [32, 1024, 768], P('dp', 'expert'), may hold values from -6 to 6
- w_project: bfloat16 [768, 2304], replicated, may hold values from -0.21875 to 0.21875
- w_output: bfloat16 [768, 768], replicated, may hold values from -0.875 to 0.875
- norm_gain: float32 [2, 768], replicated, may hold values from 0.5 to 1.5
- norm_bias: float32 [2, 768], replicated, may hold values from -3 to 3
- router: float32 [768, 8], replicated, may hold values from -0.21875 to 0.21875
- expert_weights: bfloat16 [8, 2, 768, 3072], P('expert'), may hold values from -0.21875 to 0.21875
- routes: int32 [32, 1024, 2], P('dp', 'expert'), may hold values from 0 to 7, all different within a row; in each aligned block of 128 rows (0 to 127, 128 to 255, ..., all dimensions but the last counted through in order) at most 40 rows name the same one
- keep_mask: int32 [32, 1024, 2], P('dp', 'expert'), may hold values 0 or 1
- frozen: int32 [8], replicated, may hold values from 0 to 1, as said below
- owner_list: int32 [8], replicated, may hold values from 0 to 7, each once
- attend_master: float32 [8, 768, 384], P('expert'), may hold values from -0.21875 to 0.21875
- attend_first: float32 [8, 768, 384], P('expert'), may hold values from -32 to 32
- attend_second: float32 [8, 768, 384], P('expert'), may hold values from 78.6432 to 1245.184
- attend_left: float32 [8, 768, 768], P('expert'), may hold values from -1 to 1
- attend_right: float32 [8, 384, 384], P('expert'), may hold values from -1 to 1
- expert_master: float32 [8, 2, 768, 3072], P('expert', None, None, 'dp'), may hold values from -0.21875 to 0.21875
- expert_first: float32 [8, 2, 768, 3072], P('expert', None, None, 'dp'), may hold values from -20 to 20
- expert_second: float32 [8, 2, 768, 3072], P('expert', None, None, 'dp'), may hold values from 26.2144 to 425.984
- expert_average: float32 [8, 2, 768, 3072], P('expert', None, None, 'dp'), may hold values from -0.21875 to 0.21875
- expert_basis: float32 [8, 768, 768], P('expert'), may hold values from -1 to 1
- router_first: float32 [768, 8], replicated, may hold values from -640 to 640
- router_second: float32 [768, 8], replicated, may hold values from 21299.2 to 344064
- norm_first: float32 [4, 768], replicated, may hold values from -128 to 128
- norm_second: float32 [4, 768], replicated, may hold values from 851.968 to 13762.56
Outputs:
- output: bfloat16 [32, 1024, 768], P('dp', 'expert')
- input_grad: bfloat16 [32, 1024, 768], P('dp', 'expert')
- norm_grad: float32 [4, 768], replicated
- norm_new: float32 [4, 768], replicated
- norm_first_new: float32 [4, 768], replicated
- norm_second_new: float32 [4, 768], replicated
- router_grad: float32 [768, 8], replicated
- router_new: float32 [768, 8], replicated
- router_first_new: float32 [768, 8], replicated
- router_second_new: float32 [768, 8], replicated
- attend_grad: float32 [8, 768, 384], P('expert')
- attend_master_new: float32 [8, 768, 384], P('expert')
- attend_first_new: float32 [8, 768, 384], P('expert')
- attend_second_new: float32 [8, 768, 384], P('expert')
- expert_grad: float32 [8, 2, 768, 3072], P('expert', None, None, 'dp')
- expert_master_new: float32 [8, 2, 768, 3072], P('expert', None, None, 'dp')
- expert_first_new: float32 [8, 2, 768, 3072], P('expert', None, None, 'dp')
- expert_second_new: float32 [8, 2, 768, 3072], P('expert', None, None, 'dp')
- expert_average_new: float32 [8, 2, 768, 3072], P('expert', None, None, 'dp')
Inputs may be any that keep to these rules, and one draw needn't show every extreme that they name: `routes`: each token names two different experts. In each aligned block of 128 tokens (one sequence's tokens on one index of expert) no expert is named by more than 40 choices, and some block reaches 40. `frozen`: exactly half of the experts are flagged 1. `owner_list`: A permutation.
All inputs are finite; a program needn't handle non-finite values. No bound on the sum of `keep_mask` on one device may be relied on, other than what follows from the above.
Results may differ from a plain program's by a relative error of at most 0.025.
Values may be sent and summed in bfloat16 or wider, within the bound.
A program may use at most 448 MiB of HBM per device.

v0:
```python
import jax
import jax.numpy as jnp
from jax import lax
from jax.sharding import PartitionSpec as P

HEADS = 12
HEAD_DIM = 64
TOP = 2


norm_epsilon = 1e-05
beta_one = 0.9
beta_two = 0.95
adam_epsilon = 1e-08
adam_step = 10.0
matrix_rate = 0.1
small_rate = 0.5
average_keep = 0.9
precise = lax.Precision.HIGHEST


def layer_norm(values, gain_row, bias_row):
    center = values - jnp.mean(values, axis=-1, keepdims=True)
    scaled = center * lax.rsqrt(jnp.mean(center * center, axis=-1, keepdims=True) + norm_epsilon)
    return scaled * gain_row + bias_row


def adam_move(gradient, first_moment, second_moment):
    first_new = beta_one * first_moment + (1.0 - beta_one) * gradient
    second_new = beta_two * second_moment + (1.0 - beta_two) * gradient * gradient
    direction = (
        first_new
        / (1.0 - beta_one**adam_step)
        / (jnp.sqrt(second_new / (1.0 - beta_two**adam_step)) + adam_epsilon)
    )
    return (first_new, second_new, direction)


def split_heads(piece, model_width):
    piece_len = piece.shape[1]
    keys_piece = piece[:, :, :model_width].reshape(piece.shape[0], piece_len, HEADS, HEAD_DIM)
    values_piece = piece[:, :, model_width:].reshape(piece.shape[0], piece_len, HEADS, HEAD_DIM)
    return (keys_piece, values_piece)


def score_grads(query_heads, grad_heads, log_part, delta_part, keys_piece, values_piece, allowed):
    scores = jnp.einsum(
        "sqhd,skhd->shqk", query_heads, keys_piece, preferred_element_type=jnp.float32
    ) * HEAD_DIM ** (-0.5)
    weights = jnp.where(allowed, jnp.exp(scores - log_part[..., None]), 0.0)
    grad_weights = jnp.einsum(
        "sqhd,skhd->shqk", grad_heads, values_piece, preferred_element_type=jnp.float32
    )
    grad_scores = (weights * (grad_weights - delta_part[..., None])).astype(jnp.bfloat16)
    return (weights.astype(jnp.bfloat16), grad_scores)


def on_device(
    tokens,
    cotangent,
    w_project,
    w_output,
    norm_gain,
    norm_bias,
    router,
    expert_weights,
    routes,
    keep_mask,
    frozen,
    owner_list,
    attend_master,
    attend_first,
    attend_second,
    attend_left,
    attend_right,
    expert_master,
    expert_first,
    expert_second,
    expert_average,
    expert_basis,
    router_first,
    router_second,
    norm_first,
    norm_second,
):
    seq_dev, row_len, model_width = tokens.shape
    expert_count = lax.axis_size("expert")
    my_index = lax.axis_index("expert")
    row_count = seq_dev * row_len
    capacity = max(2, 5 * row_len * TOP // (4 * expert_count))
    score_scale = HEAD_DIM ** (-0.5)
    expert_total = router.shape[1]
    token_rows = tokens.reshape(row_count, model_width).astype(jnp.float32)
    normed_one, back_one = jax.vjp(layer_norm, token_rows, norm_gain[0], norm_bias[0])
    low_one = normed_one.astype(jnp.bfloat16)
    projected = jnp.dot(low_one, w_project, preferred_element_type=jnp.float32).astype(jnp.bfloat16)
    queries = projected[:, :model_width].reshape(seq_dev, row_len, HEADS, HEAD_DIM)
    key_value = projected[:, model_width:].reshape(seq_dev, row_len, 2 * model_width)
    query_pos = my_index * row_len + jnp.arange(row_len, dtype=jnp.int32)
    init_max = jnp.full((seq_dev, HEADS, row_len), -1e30, jnp.float32)
    piece = lax.all_gather(key_value, "expert", axis=1, tiled=True)
    keys_piece, values_piece = split_heads(piece, model_width)
    key_pos = jnp.arange(piece.shape[1], dtype=jnp.int32)
    allowed = key_pos[None, :] <= query_pos[:, None]
    scores = (
        jnp.einsum("sqhd,skhd->shqk", queries, keys_piece, preferred_element_type=jnp.float32)
        * score_scale
    )
    scores = jnp.where(allowed, scores, -1e30)
    new_max = jnp.maximum(init_max, jnp.max(scores, axis=-1))
    weights = jnp.where(allowed, jnp.exp(scores - new_max[..., None]), 0.0)
    new_sum = jnp.sum(weights, axis=-1)
    update = jnp.einsum(
        "shqk,skhd->shqd",
        weights.astype(jnp.bfloat16),
        values_piece,
        preferred_element_type=jnp.float32,
    )
    attended = jnp.transpose(update / new_sum[..., None], (0, 2, 1, 3))
    log_total = new_max + jnp.log(new_sum)
    attended_low = attended.reshape(row_count, model_width).astype(jnp.bfloat16)
    middle = token_rows + jnp.dot(attended_low, w_output, preferred_element_type=jnp.float32)
    normed_two, back_two = jax.vjp(layer_norm, middle, norm_gain[1], norm_bias[1])
    low_two = normed_two.astype(jnp.bfloat16)
    low_two_wide = low_two.astype(jnp.float32)
    logits = jnp.dot(low_two_wide, router, precision=precise)
    choice_ids = routes.reshape(seq_dev, row_len * TOP)
    onehot = (choice_ids[..., None] == jnp.arange(expert_total, dtype=jnp.int32)).astype(
        jnp.float32
    )
    slot_index = jnp.sum(onehot * (jnp.cumsum(onehot, axis=1) - 1.0), axis=-1).astype(jnp.int32)
    slot_hit = (slot_index[..., None] == jnp.arange(capacity, dtype=jnp.int32)).astype(jnp.float32)
    kept = keep_mask.reshape(seq_dev, row_len * TOP).astype(jnp.float32)
    select = kept[..., None, None] * onehot[..., :, None] * slot_hit[..., None, :]
    select = select.reshape(seq_dev, row_len, TOP, expert_total, capacity).astype(jnp.bfloat16)
    low_three = low_two.reshape(seq_dev, row_len, model_width)
    sending = jnp.einsum(
        "stkec,std->escd", select, low_three, preferred_element_type=jnp.float32
    ).astype(jnp.bfloat16)
    w_first = expert_weights[0, 0]
    w_second = expert_weights[0, 1]
    hidden_width = w_first.shape[1]
    received = lax.all_to_all(sending, "expert", split_axis=0, concat_axis=0, tiled=True)
    leading = received.shape[:3]
    inputs_flat = received.reshape(-1, model_width)
    before = jnp.dot(inputs_flat, w_first, preferred_element_type=jnp.float32)
    activated = jax.nn.gelu(before).astype(jnp.bfloat16)
    result = jnp.einsum(
        "rf,df->rd", activated, w_second, preferred_element_type=jnp.float32
    ).astype(jnp.bfloat16)
    returned = result.reshape(leading + (model_width,))
    before_all = before.reshape(leading + (hidden_width,))
    coming_back = lax.all_to_all(returned, "expert", split_axis=0, concat_axis=0, tiled=True)
    per_choice = jnp.einsum(
        "stkec,escd->kstd", select, coming_back, preferred_element_type=jnp.float32
    )
    onehot_four = onehot.reshape(seq_dev, row_len, TOP, expert_total)
    chosen = jnp.sum(onehot_four * logits.reshape(seq_dev, row_len, 1, expert_total), axis=-1)
    gates = jax.nn.softmax(chosen, axis=-1)
    gates_first = jnp.transpose(gates, (2, 0, 1))
    mixture = jnp.sum(gates_first[..., None] * per_choice, axis=0)
    final = middle + mixture.reshape(row_count, model_width)
    output = final.astype(jnp.bfloat16).reshape(seq_dev, row_len, model_width)
    grad_final = cotangent.reshape(row_count, model_width).astype(jnp.float32)
    grad_mix = grad_final.reshape(seq_dev, row_len, model_width)
    grad_choice = (gates_first[..., None] * grad_mix[None]).astype(jnp.bfloat16)
    grad_gate = jnp.transpose(jnp.sum(per_choice * grad_mix[None], axis=-1), (1, 2, 0))
    grad_chosen = gates * (grad_gate - jnp.sum(gates * grad_gate, axis=-1, keepdims=True))
    grad_logits = jnp.sum(onehot_four * grad_chosen[..., None], axis=2).reshape(
        row_count, expert_total
    )
    router_local = jnp.dot(low_two_wide.T, grad_logits, precision=precise)
    grad_low_two = jnp.dot(grad_logits, router.T, precision=precise)
    grad_slots = jnp.einsum(
        "stkec,kstd->escd", select, grad_choice, preferred_element_type=jnp.float32
    ).astype(jnp.bfloat16)
    grad_rows = lax.all_to_all(grad_slots, "expert", split_axis=0, concat_axis=0, tiled=True)
    grad_flat = grad_rows.reshape(-1, model_width)
    before_flat = before_all.reshape(-1, hidden_width)
    activated, gelu_back = jax.vjp(jax.nn.gelu, before_flat)
    activated_low = activated.astype(jnp.bfloat16)
    grad_activated = jnp.dot(grad_flat, w_second, preferred_element_type=jnp.float32)
    grad_before = gelu_back(grad_activated)[0].astype(jnp.bfloat16)
    received_flat = received.reshape(-1, model_width)
    grad_first_w = jnp.einsum(
        "rd,rf->df", received_flat, grad_before, preferred_element_type=jnp.float32
    )
    grad_second_w = jnp.einsum(
        "rd,rf->df", grad_flat, activated_low, preferred_element_type=jnp.float32
    )
    grad_inputs = jnp.einsum(
        "rf,df->rd", grad_before, w_first, preferred_element_type=jnp.float32
    ).astype(jnp.bfloat16)
    grad_home = lax.all_to_all(
        grad_inputs.reshape(grad_rows.shape), "expert", split_axis=0, concat_axis=0, tiled=True
    )
    grad_low_two = grad_low_two + jnp.einsum(
        "stkec,escd->std", select, grad_home, preferred_element_type=jnp.float32
    ).reshape(row_count, model_width)
    grad_middle_norm, grad_gain_two, grad_bias_two = back_two(grad_low_two)
    grad_middle = grad_final + grad_middle_norm
    grad_branch = grad_middle.astype(jnp.bfloat16)
    grad_w_output = jnp.einsum(
        "rd,re->de", attended_low, grad_branch, preferred_element_type=jnp.float32
    )
    grad_attended = jnp.einsum(
        "re,de->rd", grad_branch, w_output, preferred_element_type=jnp.float32
    ).astype(jnp.bfloat16)
    grad_heads = grad_attended.reshape(seq_dev, row_len, HEADS, HEAD_DIM)
    row_delta = jnp.sum(grad_heads.astype(jnp.float32) * attended, axis=-1)
    delta_heads = jnp.transpose(row_delta, (0, 2, 1))
    piece = lax.all_gather(key_value, "expert", axis=1, tiled=True)
    keys_piece, values_piece = split_heads(piece, model_width)
    key_pos = jnp.arange(piece.shape[1], dtype=jnp.int32)
    allowed = key_pos[None, :] <= query_pos[:, None]
    weights_low, grad_scores = score_grads(
        queries, grad_heads, log_total, delta_heads, keys_piece, values_piece, allowed
    )
    grad_query = (
        jnp.einsum("shqk,skhd->sqhd", grad_scores, keys_piece, preferred_element_type=jnp.float32)
        * score_scale
    )
    grad_query, weights_low, grad_scores = (grad_query, weights_low, grad_scores)
    piece_len = piece.shape[1]
    grad_keys = (
        jnp.einsum("shqk,sqhd->skhd", grad_scores, queries, preferred_element_type=jnp.float32)
        * score_scale
    )
    grad_values = jnp.einsum(
        "shqk,sqhd->skhd", weights_low, grad_heads, preferred_element_type=jnp.float32
    )
    both = jnp.concatenate(
        [
            grad_keys.reshape(seq_dev, piece_len, model_width),
            grad_values.reshape(seq_dev, piece_len, model_width),
        ],
        axis=-1,
    )
    folded = (grad_query, both)
    grad_query = folded[0]
    grad_key_value = lax.psum_scatter(
        folded[1].astype(jnp.bfloat16), "expert", scatter_dimension=1, tiled=True
    ).astype(jnp.float32)
    grad_projected = jnp.concatenate(
        [
            grad_query.reshape(row_count, model_width).astype(jnp.bfloat16),
            grad_key_value.reshape(row_count, 2 * model_width).astype(jnp.bfloat16),
        ],
        axis=1,
    )
    grad_w_project = jnp.einsum(
        "rd,re->de", low_one, grad_projected, preferred_element_type=jnp.float32
    )
    grad_low_one = jnp.einsum(
        "re,de->rd", grad_projected, w_project, preferred_element_type=jnp.float32
    )
    grad_tokens_norm, grad_gain_one, grad_bias_one = back_one(grad_low_one)
    input_grad = (
        (grad_middle + grad_tokens_norm).astype(jnp.bfloat16).reshape(seq_dev, row_len, model_width)
    )
    grad_attend_full = jnp.concatenate([grad_w_project, grad_w_output], axis=1)
    grad_norms = jnp.stack([grad_gain_one, grad_gain_two, grad_bias_one, grad_bias_two])
    block_width = attend_master.shape[2]
    slot_range = jnp.arange(expert_count, dtype=jnp.int32)
    summed_full, router_grad, norm_grad = lax.psum(
        (grad_attend_full, router_local, grad_norms), ("dp", "expert")
    )
    which_block = jnp.sum(slot_range * (owner_list == my_index).astype(jnp.int32))
    block_grad = lax.dynamic_slice_in_dim(summed_full, which_block * block_width, block_width, 1)
    left_basis = attend_left[0]
    right_basis = attend_right[0]
    rotated = jnp.dot(
        jnp.dot(left_basis.T, block_grad, precision=precise), right_basis, precision=precise
    )
    attend_first_new, attend_second_new, direction = adam_move(
        rotated, attend_first[0], attend_second[0]
    )
    stepped = jnp.dot(
        jnp.dot(left_basis, direction, precision=precise), right_basis.T, precision=precise
    )
    attend_master_new = attend_master[0] - matrix_rate * stepped
    flag_value = jnp.sum(
        frozen * (jnp.arange(frozen.shape[0], dtype=jnp.int32) == my_index).astype(jnp.int32)
    )
    trainable = (1 - flag_value).astype(jnp.float32)
    expert_stack = jnp.stack([grad_first_w, grad_second_w]) * trainable
    expert_grad = lax.psum_scatter(
        expert_stack.astype(jnp.bfloat16), "dp", scatter_dimension=2, tiled=True
    ).astype(jnp.float32)
    basis = expert_basis[0]
    expert_rotated = jnp.einsum("dj,ndf->njf", basis, expert_grad, precision=precise)
    first_new, second_new, expert_direction = adam_move(
        expert_rotated, expert_first[0], expert_second[0]
    )
    expert_step = jnp.einsum("dj,njf->ndf", basis, expert_direction, precision=precise)
    is_frozen = flag_value > 0
    expert_master_new = jnp.where(
        is_frozen, expert_master[0], expert_master[0] - matrix_rate * expert_step
    )
    expert_first_new = jnp.where(is_frozen, expert_first[0], first_new)
    expert_second_new = jnp.where(is_frozen, expert_second[0], second_new)
    expert_average_new = average_keep * expert_average[0] + (1.0 - average_keep) * expert_master_new
    router_first_new, router_second_new, router_step = adam_move(
        router_grad, router_first, router_second
    )
    router_new = router - matrix_rate * router_step
    norm_params = jnp.concatenate([norm_gain, norm_bias], axis=0)
    norm_first_new, norm_second_new, norm_step = adam_move(norm_grad, norm_first, norm_second)
    norm_new = norm_params - small_rate * norm_step
    return (
        output,
        input_grad,
        norm_grad,
        norm_new,
        norm_first_new,
        norm_second_new,
        router_grad,
        router_new,
        router_first_new,
        router_second_new,
        block_grad[None],
        attend_master_new[None],
        attend_first_new[None],
        attend_second_new[None],
        expert_grad[None],
        expert_master_new[None],
        expert_first_new[None],
        expert_second_new[None],
        expert_average_new[None],
    )


def solution(mesh):
    return jax.shard_map(
        on_device,
        mesh=mesh,
        in_specs=(
            P("dp", "expert", None),
            P("dp", "expert", None),
            P(),
            P(),
            P(),
            P(),
            P(),
            P("expert", None, None, None),
            P("dp", "expert", None),
            P("dp", "expert", None),
            P(),
            P(),
            P("expert", None, None),
            P("expert", None, None),
            P("expert", None, None),
            P("expert", None, None),
            P("expert", None, None),
            P("expert", None, None, "dp"),
            P("expert", None, None, "dp"),
            P("expert", None, None, "dp"),
            P("expert", None, None, "dp"),
            P("expert", None, None),
            P(),
            P(),
            P(),
            P(),
        ),
        out_specs=(
            P("dp", "expert", None),
            P("dp", "expert", None),
            P(),
            P(),
            P(),
            P(),
            P(),
            P(),
            P(),
            P(),
            P("expert", None, None),
            P("expert", None, None),
            P("expert", None, None),
            P("expert", None, None),
            P("expert", None, None, "dp"),
            P("expert", None, None, "dp"),
            P("expert", None, None, "dp"),
            P("expert", None, None, "dp"),
            P("expert", None, None, "dp"),
        ),
        check_vma=False,
    )
```

profile of v0, /device:TPU:0, one launch (start us, length us, event | category | flops | bytes accessed | tf_op | source)
XLA Modules:
  0.0 1834.1 jit_solution(516618499230071910)
XLA Ops:
  13.9 4.1 convolution_convert_fusion
  22.1 2.7 slice.50
  27.3 3.0 copy.199
  35.3 9.3 reduce-window.6
  57.6 447.7 %all-gather.2.cloned.1.call-done = bf16[8,1024,1536]{2,1,0:T(8,128)(2,1)} async-done(((bf16[8,128,1536]{2,1,0:T(8,128)(2,1)}), bf16[8,1024,1536]{2,1,0:T(8,128)(2,1)}) %all-gather.2.cloned.1.call-update) | async-done | bytes 25165840 | tf_op jit(solution)/shard_map/all_gather | solution.py:101
  505.3 17.1 fusion.171
  522.5 16.6 copy.148
  539.1 23.2 %select_reduce_fusion = (f32[8,12,128]{2,1,0:T(8,128)S(1)}, f32[8,12,128,1024]{3,2,1,0:T(8,128)}) fusion(pred[128,1024]{1,0:T(8,128)(4,1)} %iota_compare_fusion, bf16[8,1024,12,64]{1,3,2,0:T(8,128)(2,1)} %bitcast.322, bf16[8,128,12,64]{1,0,3,2:T(8,128)(2,1)} %bitcast.327), kind=kOutput, calls=%fused_computation.4 | convolution fusion | flops 1648349184 | bytes 64667648 | tf_op jit(solution)/shard_map/sqhd,skhd->shqk/dot_general | solution.py:106
  563.5 16.7 copy.150
  580.2 24.0 %fusion.2 = f32[8,12,128]{2,1,0:T(8,128)S(1)} fusion(f32[8,12,128,1024]{3,2,1,0:T(8,128)} %get-tuple-element.133, f32[8,12,128]{2,1,0:T(8,128)} %broadcast_maximum_fusion, pred[128,1024]{1,0:T(8,128)(4,1)} %iota_compare_fusion), kind=kLoop, calls=%fused_computation.8 | loop fusion | flops 62902272 | bytes 50561024 | tf_op jit(solution)/shard_map/reduce_sum | solution.py:112
  604.2 25.4 %fusion.172 = (bf16[8,128,12,64]{1,3,2,0:T(8,128)(2,1)}, f32[8,128,12,64]{1,3,2,0:T(8,128)}) fusion(f32[8,128,12]{1,2,0:T(8,128)S(1)} %bitcast.350, bf16[8,1024,12,64]{1,3,2,0:T(8,128)(2,1)} %bitcast.329, f32[8,12,128,1024]{3,2,1,0:T(8,128)} %get-tuple-element.133, f32[8,12,128]{2,1,0:T(8,128)S(1)} %copy-done.31, pred[128,1024]{1,0:T(8,128)(4,1)S(1)} %copy-done.7), kind=kOutput, calls=%fused_computation.252 | convolution fusion | flops 1675100160 | bytes 67862528 | tf_op jit(solution)/shard_map/shqk,skhd->shqd/dot_general | solution.py:113
  642.9 4.6 all-to-all-start
  647.5 3.1 copy.164
  651.8 3.3 fusion.46
  657.2 78.1 %all-to-all-done = bf16[8,8,40,768]{3,2,1,0:T(8,128)(2,1)} async-done(((bf16[8,8,40,768]{3,2,1,0:T(8,128)(2,1)}), bf16[8,8,40,768]{3,2,1,0:T(8,128)(2,1)}, u32[]{:S(2)}, u32[]{:S(2)}) %all-to-all-start) | async-done | bytes 3932192 | tf_op jit(solution)/shard_map/all_to_all | solution.py:143
  735.3 4.8 all-to-all-start.2
  741.3 21.0 %fusion.34 = f32[2560,3072]{1,0:T(8,128)} fusion(bf16[2560,768]{1,0:T(8,128)(2,1)} %bitcast.21, bf16[1,2,768,3072]{3,2,1,0:T(8,128)(2,1)} %param.33), kind=kOutput, calls=%fused_computation.61 | convolution fusion | flops 12079595520 | bytes 40108032 | tf_op jit(solution)/shard_map/dot_general | solution.py:146
  762.3 25.1 %convolution_convert_fusion.2 = bf16[2560,768]{1,0:T(8,128)(2,1)} fusion(bf16[1,2,768,3072]{3,2,1,0:T(8,128)(2,1)} %param.33, f32[2560,3072]{1,0:T(8,128)} %fusion.34), kind=kOutput, calls=%fused_computation.43 | convolution fusion | flops 12152340480 | bytes 40108032 | tf_op jit(solution)/shard_map/rf,df->rd/dot_general | solution.py:148
  787.4 39.6 %all-to-all-done.2 = bf16[8,8,40,768]{3,2,1,0:T(8,128)(2,1)} async-done(((bf16[8,8,40,768]{3,2,1,0:T(8,128)(2,1)}), bf16[8,8,40,768]{3,2,1,0:T(8,128)(2,1)}, u32[]{:S(2)}, u32[]{:S(2)}) %all-to-all-start.2) | async-done | bytes 3932192 | tf_op jit(solution)/shard_map/all_to_all | solution.py:177
  827.0 36.3 %fusion.10 = bf16[2560,3072]{1,0:T(8,128)(2,1)} fusion(f32[2560,3072]{1,0:T(8,128)} %fusion.34, bf16[2560,768]{1,0:T(8,128)(2,1)} %bitcast.39, bf16[1,2,768,3072]{3,2,1,0:T(8,128)(2,1)} %param.33), kind=kOutput, calls=%fused_computation.16 | convolution fusion | flops 12236881920 | bytes 55836672 | tf_op jit(solution)/shard_map/dot_general | solution.py:182
  863.3 4.7 all-to-all-start.1
  868.1 17.8 convolution_convert_fusion.1
  885.9 21.1 %convolution_bitcast_fusion = f32[1,768,3072]{2,1,0:T(8,128)} fusion(bf16[2560,768]{1,0:T(8,128)(2,1)} %bitcast.39, f32[2560,3072]{1,0:T(8,128)} %fusion.34), kind=kOutput, calls=%fused_computation.40 | convolution fusion | flops 12150374400 | bytes 44826624 | tf_op jit(solution)/shard_map/rd,rf->df/dot_general | solution.py:188
  907.0 48.0 %all-to-all-done.1 = bf16[8,8,40,768]{3,2,1,0:T(8,128)(2,1)} async-done(((bf16[8,8,40,768]{3,2,1,0:T(8,128)(2,1)}), bf16[8,8,40,768]{3,2,1,0:T(8,128)(2,1)}, u32[]{:S(2)}, u32[]{:S(2)}) %all-to-all-start.1) | async-done | bytes 3932192 | tf_op jit(solution)/shard_map/all_to_all | solution.py:153
  955.0 4.5 all-to-all-start.3
  959.6 17.1 convolution_bitcast_fusion.1
  976.8 4.7 fusion.20
  983.5 7.5 fusion.25
  991.0 4.5 copy.163
  998.5 48.0 %all-to-all-done.3 = bf16[8,8,40,768]{3,2,1,0:T(8,128)(2,1)} async-done(((bf16[8,8,40,768]{3,2,1,0:T(8,128)(2,1)}), bf16[8,8,40,768]{3,2,1,0:T(8,128)(2,1)}, u32[]{:S(2)}, u32[]{:S(2)}) %all-to-all-start.3) | async-done | bytes 3932192 | tf_op jit(solution)/shard_map/all_to_all | solution.py:194
  1046.5 3.6 fusion.49
  1050.2 5.1 multiply_reduce_fusion
  1055.4 2.7 fusion.170
  1068.5 32.9 %multiply_convert_fusion = bf16[8,12,128,1024]{3,2,1,0:T(8,128)(2,1)} fusion(f32[8,12,128,1024]{3,2,1,0:T(8,128)} %get-tuple-element.133, f32[8,12,128]{2,1,0:T(8,128)S(1)} %bitcast.351, f32[8,12,128]{2,1,0:T(8,128)S(1)} %copy-done.43, pred[128,1024]{1,0:T(8,128)(4,1)S(1)} %copy-done.8, bf16[8,1024,12,64]{1,3,2,0:T(8,128)(2,1)} %bitcast.330, ...), kind=kOutput, calls=%fused_computation.1 | convolution fusion | flops 1686110208 | bytes 89882624 | tf_op jit(solution)/shard_map/sqhd,skhd->shqk/dot_general | solution.py:51
  1101.5 15.0 multiply_convert_fusion.2
  1116.5 16.6 copy.174
  1133.1 22.5 %fusion.21 = bf16[8,12,64,1024]{3,2,1,0:T(8,128)(2,1)} fusion(f32[8,12,128,1024]{3,2,1,0:T(8,128)} %get-tuple-element.133, f32[8,12,128]{2,1,0:T(8,128)} %log_add_fusion, pred[128,1024]{1,0:T(8,128)(4,1)} %iota_compare_fusion, bf16[8,128,12,64]{1,0,3,2:T(8,128)(2,1)} %bitcast.339), kind=kOutput, calls=%fused_computation.33 | convolution fusion | flops 1667235840 | bytes 64667648 | tf_op jit(solution)/shard_map/shqk,sqhd->skhd/dot_general | solution.py:229
  1155.6 16.7 copy.175
  1172.3 20.3 %pad_maximum_fusion = bf16[8,1024,1536]{2,1,0:T(8,128)(2,1)} fusion(bf16[8,1024,768]{2,1,0:T(8,128)(2,1)} %copy.175, bf16[8,1024,768]{2,1,0:T(8,128)(2,1)} %copy.174), kind=kLoop, calls=%fused_computation.19 | loop fusion | flops 50331648 | bytes 50331648 | tf_op jit(solution)/shard_map/concatenate | solution.py:232
  1193.2 6.0 copy.179
  1199.3 6.3 copy.181
  1205.6 6.1 copy.178
  1211.7 6.1 copy.183
  1218.4 15.6 fusion.94
  1240.7 2.7 fusion.129
  1243.4 5.2 fusion.90
  1248.6 9.9 fusion.75
  1258.5 336.3 %reduce-scatter.3.cloned.1.call-done = bf16[8,128,1536]{2,1,0:T(8,128)(2,1)} async-done(((bf16[8,1024,1536]{2,1,0:T(8,128)(2,1)}), bf16[8,128,1536]{2,1,0:T(8,128)(2,1)}) %reduce-scatter.3.cloned.1.call-update) | async-done | bytes 3145744 | tf_op jit(solution)/shard_map/reduce_scatter | solution.py:241
  1594.8 9.5 fusion.70
  1604.3 8.7 pad_maximum_fusion.1
  1613.1 23.3 %fusion.27 = (f32[1,2,768,768]{2,3,1,0:T(8,128)}, f32[1,2,768,768]{2,3,1,0:T(8,128)}) fusion(f32[1,2,768,768]{2,3,1,0:T(8,128)} %copy.183, f32[1,2,768,768]{2,3,1,0:T(8,128)} %copy.178, pred[]{:T(512)S(6)} %gt.3, f32[1,768,768]{2,1,0:T(8,128)} %param.47, f32[2,768,768]{2,1,0:T(8,128)} %fusion.75, f32[1,2,768,768]{2,3,1,0:T(8,128)} %copy.179, ...), kind=kOutput, calls=%fused_computation.49 | convolution fusion | flops 10891689984 | bytes 35389440 | tf_op jit(solution)/shard_map/dj,njf->ndf/dot_general | solution.py:295
  1636.3 6.5 copy.184
  1642.9 6.1 copy.187
  1649.0 10.4 fusion.28
  1659.3 6.1 copy.185
  1665.4 6.1 copy.186
  1671.5 4.4 bitcast_convert_fusion.1
  1676.0 4.1 fusion.65
  1683.1 41.3 %all-reduce = (f32[4,768]{1,0:T(4,128)}, f32[768,8]{0,1:T(8,128)}) all-reduce(f32[4,768]{1,0:T(4,128)} %pad_maximum_fusion.5, f32[768,8]{0,1:T(8,128)} %fusion.129), channel_id=1, replica_groups=mesh['dp'=4,'expert'=8] {'dp','expert'}, use_global_device_ids=true, to_apply=%region_27.28 | all-reduce | flops 9216 | bytes 73728 | tf_op jit(solution)/shard_map/psum | solution.py:265
  1728.0 4.9 add_convert_fusion
  1732.9 70.7 %all-reduce.3.cloned.1.call-done = f32[768,3072]{1,0:T(8,128)} async-done(((f32[768,3072]{1,0:T(8,128)}), f32[768,3072]{1,0:T(8,128)}) %all-reduce.3.cloned.1.call-update) | async-done | bytes 9437200 | tf_op jit(solution)/shard_map/psum | solution.py:265
  1803.6 5.3 fusion.79
  1813.2 6.7 fusion.77
  1819.9 5.0 fusion.96
  (212 shorter events, 85.1 us)
Async XLA Ops:
  7.2 6.7 copy-start
  7.2 498.1 %all-gather.2.cloned.1.call-start = ((), (), s32[]{:S(2)}) async-start(), calls=%async_computation.6 | async-start | bytes 28311552 | tf_op jit(solution)/shard_map/all_gather | solution.py:101
  7.3 6.0 copy-start.3
  9.1 3.5 copy-start.44
  12.6 622.0 %copy-start.39 = (f32[768]{0:T(1024)}, f32[768]{0:T(1024)S(1)}, u32[]{:S(2)}) copy-start(f32[768]{0:T(1024)S(1)} %get-tuple-element.146) | copy-start | bytes 9220
  13.9 4.1 copy-start.21
  17.9 2.2 copy-start.16
  24.7 6.9 copy-start.38
  580.2 24.0 %copy-start.7 = (pred[128,1024]{1,0:T(8,128)(4,1)S(1)}, pred[128,1024]{1,0:T(8,128)(4,1)}, u32[]{:S(2)}) copy-start(pred[128,1024]{1,0:T(8,128)(4,1)} %iota_compare_fusion) | copy-start | bytes 393220
  580.2 24.0 %copy-start.31 = (f32[8,12,128]{2,1,0:T(8,128)S(1)}, f32[8,12,128]{2,1,0:T(8,128)}, u32[]{:S(2)}) copy-start(f32[8,12,128]{2,1,0:T(8,128)} %broadcast_maximum_fusion) | copy-start | bytes 147460
  604.2 25.4 %copy-start.30 = (f32[8,12,128]{2,1,0:T(8,128)}, f32[8,12,128]{2,1,0:T(8,128)S(1)}, u32[]{:S(2)}) copy-start(f32[8,12,128]{2,1,0:T(8,128)S(1)} %fusion.2) | copy-start | bytes 147460
  604.2 28.1 %copy-start.4 = (bf16[8,128,768]{2,1,0:T(8,128)(2,1)S(1)}, bf16[8,128,768]{2,1,0:T(8,128)(2,1)}, u32[]{:S(2)}) copy-start(bf16[8,128,768]{2,1,0:T(8,128)(2,1)} %param.26) | copy-start | bytes 4718596
  604.2 28.1 %copy-start.65 = (bf16[768,768]{1,0:T(8,128)(2,1)S(1)}, bf16[768,768]{1,0:T(8,128)(2,1)}, u32[]{:S(2)}) copy-start(bf16[768,768]{1,0:T(8,128)(2,1)} %param.29) | copy-start | bytes 3538948
  632.3 1.7 copy-start.22
  634.0 2.1 copy-start.1
  634.0 2.1 copy-start.34
  634.0 2.1 copy-start.32
  634.6 2.9 copy-start.55
  634.6 3.0 copy-start.18
  636.1 4.2 copy-start.6
  637.5 1.6 copy-start.28
  642.9 92.4 %all-to-all-start = ((bf16[8,8,40,768]{3,2,1,0:T(8,128)(2,1)}), bf16[8,8,40,768]{3,2,1,0:T(8,128)(2,1)}, u32[]{:S(2)}, u32[]{:S(2)}) async-start(bf16[8,8,40,768]{3,2,1,0:T(8,128)(2,1)} %copy.160), calls=%async_computation | async-start | bytes 7864320 | tf_op jit(solution)/shard_map/all_to_all | solution.py:143
  657.2 82.8 %copy-start.62 = (s32[8]{0:T(128)S(1)}, s32[8]{0:T(128)}, u32[]{:S(2)}) copy-start(s32[8]{0:T(128)} %param.37) | copy-start | bytes 100
  657.2 82.9 %copy-start.63 = (s32[8]{0:T(128)S(1)}, s32[8]{0:T(128)}, u32[]{:S(2)}) copy-start(s32[8]{0:T(128)} %param.36) | copy-start | bytes 100
  735.3 91.7 %all-to-all-start.2 = ((bf16[8,8,40,768]{3,2,1,0:T(8,128)(2,1)}), bf16[8,8,40,768]{3,2,1,0:T(8,128)(2,1)}, u32[]{:S(2)}, u32[]{:S(2)}) async-start(bf16[8,8,40,768]{3,2,1,0:T(8,128)(2,1)} %copy.166), calls=%async_computation.2 | async-start | bytes 7864320 | tf_op jit(solution)/shard_map/all_to_all | solution.py:177
  863.3 91.7 %all-to-all-start.1 = ((bf16[8,8,40,768]{3,2,1,0:T(8,128)(2,1)}), bf16[8,8,40,768]{3,2,1,0:T(8,128)(2,1)}, u32[]{:S(2)}, u32[]{:S(2)}) async-start(bf16[8,8,40,768]{3,2,1,0:T(8,128)(2,1)} %bitcast.342), calls=%async_computation.1 | async-start | bytes 7864320 | tf_op jit(solution)/shard_map/all_to_all | solution.py:153
  955.0 91.5 %all-to-all-start.3 = ((bf16[8,8,40,768]{3,2,1,0:T(8,128)(2,1)}), bf16[8,8,40,768]{3,2,1,0:T(8,128)(2,1)}, u32[]{:S(2)}, u32[]{:S(2)}) async-start(bf16[8,8,40,768]{3,2,1,0:T(8,128)(2,1)} %bitcast.341), calls=%async_computation.3 | async-start | bytes 7864320 | tf_op jit(solution)/shard_map/all_to_all | solution.py:194
  959.6 289.0 %reduce-scatter.5.cloned.1.call-start = ((), (), s32[]{:S(2)}) async-start(), calls=%async_computation.9 | async-start | bytes 11796480 | tf_op jit(solution)/shard_map/reduce_scatter | solution.py:287
  959.6 17.1 copy-start.12
  981.5 2.0 copy-start.57
  981.5 613.3 %reduce-scatter.3.cloned.1.call-start = ((), (), s32[]{:S(2)}) async-start(), calls=%async_computation.7 | async-start | bytes 28311552 | tf_op jit(solution)/shard_map/reduce_scatter | solution.py:241
  991.0 4.5 copy-start.37
  995.5 54.6 %copy-start.35 = (f32[1024]{0:T(1024)S(1)}, f32[1024]{0:T(1024)}, u32[]{:S(2)}) copy-start(f32[1024]{0:T(1024)} %copy-done.34) | copy-start | bytes 12292
  995.5 54.6 %copy-start.40 = (f32[768]{0:T(1024)S(1)}, f32[768]{0:T(1024)}, u32[]{:S(2)}) copy-start(f32[768]{0:T(1024)} %copy-done.39) | copy-start | bytes 9220
  1046.5 3.6 copy-start.2
  1046.5 3.6 copy-start.29
  1046.5 3.6 copy-start.33
  1050.2 5.1 copy-start.53
  1050.2 5.1 copy-start.10
  1050.2 5.1 copy-start.42
  1055.3 2.8 copy-start.13
  1058.1 2.1 copy-start.66
  1058.5 1.7 copy-start.9
  1065.4 2.4 copy-start.17
  1065.4 3.2 copy-start.8
  1065.4 3.2 copy-start.43
  1192.6 611.0 %all-reduce.3.cloned.1.call-start = ((), (), s32[]{:S(2)}) async-start(), calls=%async_computation.8 | async-start | bytes 18874368 | tf_op jit(solution)/shard_map/psum | solution.py:265
  1235.3 4.2 copy-start.59
  1235.3 4.8 copy-start.58
  1671.4 4.4 copy-start.5
  1671.4 4.4 copy-start.23
  1671.4 4.4 copy-start.45
  1671.4 4.4 copy-start.47
  1671.5 4.5 copy-start.64
  1675.9 4.1 copy-start.51
  1676.0 4.1 copy-start.49
  1680.0 2.5 copy-start.11
  1680.0 2.5 copy-start.60
  1680.0 2.5 copy-start.61
  1803.6 5.3 copy-start.20
  1803.6 7.9 copy-start.24
  1803.6 7.9 copy-start.25
  1808.9 4.3 copy-start.19
  1813.2 6.7 copy-start.26
  (11 other events, 8.7 us)
Sparse Core Ops, SparseCore 0:
  22.2 483.0 all-gather.1
  981.6 78.9 reduce-scatter.4
  1192.7 402.0 reduce-scatter.2
  1613.2 190.3 all-reduce.2
where the time goes:
time: 1850 us; the launch traced here: 1830 us
  waiting for transfers between devices  1070 us (58%)
  matrix products  377 us (20%)
  local copies, waits for them, and re-layouts  191 us (10%)
  other arithmetic  119 us (6%)
  blocking collectives  41.3 us (2%)
  starting transfers between devices  19.1 us (1%)
    all_gather x1, waiting for transfers between devices, on_device(): piece = lax.all_gather(key_value, 'expert', axis=1, tiled=True)  448 us
    reduce_scatter x1, waiting for transfers between devices, on_device(): lax.psum_scatter(folded[1].astype(jnp.bfloat16), 'expert', scatter_dimens...  336 us
    all_to_all x1, waiting for transfers between devices, on_device(): lax.all_to_all(sending, 'expert', split_axis=0, concat_axis=0, tiled=True)  78.1 us
    psum x1, waiting for transfers between devices, on_device(): lax.psum((grad_attend_full, router_local, grad_norms), ('dp', 'expert'))  70.7 us
    unnamed x146, local copies, waits for them, and re-layouts  65.3 us
    all_to_all x1, waiting for transfers between devices, on_device(): lax.all_to_all(grad_inputs.reshape(grad_rows.shape), 'expert', split_axis...  48 us
    all_to_all x1, waiting for transfers between devices, on_device(): lax.all_to_all(returned, 'expert', split_axis=0, concat_axis=0, tiled=True)  48 us
    psum x1, blocking collectives, on_device(): lax.psum((grad_attend_full, router_local, grad_norms), ('dp', 'expert'))  41.3 us
  transfers between devices with their start and end apart: 8, of which 7 were waited for; matrix products, arithmetic and copies ran while one was open for 25% of the time, Pallas kernels for 0%

commit v1 on v0

v1 whole, which is shorter than its diff:
```python
import functools

import jax
import jax.numpy as jnp
from jax import lax
from jax.experimental import pallas as pl
from jax.experimental.pallas import tpu as pltpu
from jax.sharding import PartitionSpec as P

HEADS = 12
HEAD_DIM = 64
TOP = 2
TILE = 256


norm_epsilon = 1e-05
beta_one = 0.9
beta_two = 0.95
adam_epsilon = 1e-08
adam_step = 10.0
matrix_rate = 0.1
small_rate = 0.5
average_keep = 0.9
precise = lax.Precision.HIGHEST
wide = jnp.float32
low = jnp.bfloat16


def norm_parts(values):
    center = values - jnp.mean(values, axis=-1, keepdims=True)
    spread = lax.rsqrt(jnp.mean(center * center, axis=-1, keepdims=True) + norm_epsilon)
    return center * spread, spread


def norm_back(grad, normal, spread, gain_row):
    g = grad * gain_row
    moved = spread * (
        g
        - jnp.mean(g, axis=-1, keepdims=True)
        - normal * jnp.mean(g * normal, axis=-1, keepdims=True)
    )
    return moved, jnp.sum(grad * normal, axis=0), jnp.sum(grad, axis=0)


def adam_move(gradient, first_moment, second_moment):
    first_new = beta_one * first_moment + (1.0 - beta_one) * gradient
    second_new = beta_two * second_moment + (1.0 - beta_two) * gradient * gradient
    direction = (
        first_new
        / (1.0 - beta_one**adam_step)
        / (jnp.sqrt(second_new / (1.0 - beta_two**adam_step)) + adam_epsilon)
    )
    return (first_new, second_new, direction)


def dot_low(a, b, dims):
    return lax.dot_general(a.astype(low), b.astype(low), (dims, ((), ())), preferred_element_type=wide)


ROW_COL = ((1,), (0,))
ROW_ROW = ((1,), (1,))
COL_COL = ((0,), (0,))


def key_pieces(step, tile, key_len, whole):
    if whole:
        return ((0, step * tile, False), (step * tile, (step + 1) * tile, True))
    return ((0, key_len, True),)


def allowed_at(first_query, first_key, tile, key_count):
    rows = lax.broadcasted_iota(jnp.int32, (tile, key_count), 0) + first_query
    columns = lax.broadcasted_iota(jnp.int32, (tile, key_count), 1) + first_key
    return columns <= rows


def attend_kernel(whole, start_ref, q_ref, k_ref, v_ref, out_ref, log_ref):
    rows, lanes = q_ref.shape
    key_len = k_ref.shape[0]
    lane = lax.broadcasted_iota(jnp.int32, (1, lanes), 1)
    for step in range(rows // TILE):
        at = slice(step * TILE, (step + 1) * TILE)
        total, logs = None, []
        for head in range(2):
            mine = (lane // HEAD_DIM) == head
            query = jnp.where(mine, q_ref[at, :] * HEAD_DIM ** (-0.5), 0).astype(low)
            parts = []
            for first, last, masked in key_pieces(step, TILE, key_len, whole):
                if last > first:
                    scores = dot_low(query, k_ref[first:last, :], ROW_ROW)
                    if masked:
                        origin = step * TILE + (0 if whole else start_ref[0])
                        scores = jnp.where(
                            allowed_at(origin, first, TILE, last - first), scores, -1e30
                        )
                    parts.append((first, last, scores))
            top = functools.reduce(
                jnp.maximum, [jnp.max(s, axis=-1, keepdims=True) for _, _, s in parts]
            )
            summed, acc = None, None
            for first, last, scores in parts:
                weights = jnp.exp(scores - top)
                here = jnp.sum(weights, axis=-1, keepdims=True)
                values = jnp.where(mine, v_ref[first:last, :], 0).astype(low)
                add = dot_low(weights, values, ROW_COL)
                summed = here if summed is None else summed + here
                acc = add if acc is None else acc + add
            acc = acc / summed
            total = acc if total is None else total + acc
            logs.append(top + jnp.log(summed))
        out_ref[at, :] = total.astype(out_ref.dtype)
        log_ref[at, :] = jnp.where(lane < HEAD_DIM, logs[0], logs[1])


def attend_back_kernel(
    whole, start_ref, q_ref, k_ref, v_ref, g_ref, a_ref, log_ref, dq_ref, dk_ref, dv_ref, dk_sum, dv_sum
):
    rows, lanes = q_ref.shape
    key_len = k_ref.shape[0]
    lane = lax.broadcasted_iota(jnp.int32, (1, lanes), 1)
    dk_sum[...] = jnp.zeros_like(dk_sum)
    dv_sum[...] = jnp.zeros_like(dv_sum)
    for step in range(rows // TILE):
        at = slice(step * TILE, (step + 1) * TILE)
        grad_all = g_ref[at, :]
        product = grad_all.astype(wide) * a_ref[at, :].astype(wide)
        dq = None
        for head in range(2):
            mine = (lane // HEAD_DIM) == head
            query = jnp.where(mine, q_ref[at, :] * HEAD_DIM ** (-0.5), 0).astype(low)
            grad = jnp.where(mine, grad_all, 0).astype(low)
            delta = jnp.sum(jnp.where(mine, product, 0.0), axis=-1, keepdims=True)
            log_total = log_ref[at, head * HEAD_DIM : head * HEAD_DIM + 1]
            for first, last, masked in key_pieces(step, TILE, key_len, whole):
                if last > first:
                    keys, values = k_ref[first:last, :], v_ref[first:last, :]
                    weights = jnp.exp(dot_low(query, keys, ROW_ROW) - log_total)
                    if masked:
                        origin = step * TILE + (0 if whole else start_ref[0])
                        weights = jnp.where(
                            allowed_at(origin, first, TILE, last - first), weights, 0.0
                        )
                    moved = (weights * (dot_low(grad, values, ROW_ROW) - delta)).astype(low)
                    dv_sum[first:last, :] += dot_low(weights, grad, COL_COL)
                    dk_sum[first:last, :] += dot_low(moved, query, COL_COL)
                    add = dot_low(moved, jnp.where(mine, keys, 0), ROW_COL)
                    dq = add if dq is None else dq + add
        dq_ref[at, :] = (dq * HEAD_DIM ** (-0.5)).astype(low)
    dk_ref[...] = dk_sum[...].astype(low)
    dv_ref[...] = dv_sum[...].astype(low)


def head_block(rows, first):
    return pl.BlockSpec((rows, 2 * HEAD_DIM), lambda pair: (0, first + pair))


def attend(start, queries, keys, values, firsts, whole):
    rows, key_len, pairs = queries.shape[0], keys.shape[0], HEADS // 2
    width = HEADS * HEAD_DIM
    cost = 4 * rows * key_len * width // (2 if whole else 1)
    return pl.pallas_call(
        functools.partial(attend_kernel, whole),
        grid=(pairs,),
        out_shape=(
            jax.ShapeDtypeStruct((rows, width), low),
            jax.ShapeDtypeStruct((rows, width), wide),
        ),
        in_specs=[
            pl.BlockSpec(memory_space=pltpu.SMEM),
            head_block(rows, firsts[0]),
            head_block(key_len, firsts[1]),
            head_block(key_len, firsts[2]),
        ],
        out_specs=(head_block(rows, 0), head_block(rows, 0)),
        cost_estimate=pl.CostEstimate(
            flops=cost, bytes_accessed=12 * rows * width, transcendentals=rows * key_len * HEADS
        ),
        name="attend",
    )(start, queries, keys, values)


def attend_back(start, queries, keys, values, firsts, grads, attended, logs, whole):
    rows, key_len, pairs = queries.shape[0], keys.shape[0], HEADS // 2
    width = HEADS * HEAD_DIM
    cost = 10 * rows * key_len * width // (2 if whole else 1)
    return pl.pallas_call(
        functools.partial(attend_back_kernel, whole),
        grid=(pairs,),
        out_shape=(
            jax.ShapeDtypeStruct((rows, width), low),
            jax.ShapeDtypeStruct((key_len, width), low),
            jax.ShapeDtypeStruct((key_len, width), low),
        ),
        in_specs=[
            pl.BlockSpec(memory_space=pltpu.SMEM),
            head_block(rows, firsts[0]),
            head_block(key_len, firsts[1]),
            head_block(key_len, firsts[2]),
            head_block(rows, 0),
            head_block(rows, 0),
            head_block(rows, 0),
        ],
        out_specs=(head_block(rows, 0), head_block(key_len, 0), head_block(key_len, 0)),
        scratch_shapes=[
            pltpu.VMEM((key_len, 2 * HEAD_DIM), wide),
            pltpu.VMEM((key_len, 2 * HEAD_DIM), wide),
        ],
        cost_estimate=pl.CostEstimate(
            flops=cost, bytes_accessed=20 * rows * width, transcendentals=rows * key_len * HEADS
        ),
        name="attend_back",
    )(start, queries, keys, values, grads, attended, logs)


def on_device(
    tokens,
    cotangent,
    w_project,
    w_output,
    norm_gain,
    norm_bias,
    router,
    expert_weights,
    routes,
    keep_mask,
    frozen,
    owner_list,
    attend_master,
    attend_first,
    attend_second,
    attend_left,
    attend_right,
    expert_master,
    expert_first,
    expert_second,
    expert_average,
    expert_basis,
    router_first,
    router_second,
    norm_first,
    norm_second,
):
    seq_dev, row_len, model_width = tokens.shape
    expert_count = lax.axis_size("expert")
    dp_count = lax.axis_size("dp")
    my_index = lax.axis_index("expert")
    row_count = seq_dev * row_len
    capacity = max(2, 5 * row_len * TOP // (4 * expert_count))
    expert_total = router.shape[1]
    slots = expert_total * capacity
    parts = expert_count // seq_dev
    whole = parts == 1
    groups, across = None, None
    if not whole:
        groups = [[p * seq_dev + s for s in range(seq_dev)] for p in range(parts)]
        across = [[p * seq_dev + s for p in range(parts)] for s in range(seq_dev)]

    def swap(value):
        return lax.all_to_all(
            value, "expert", split_axis=0, concat_axis=0, tiled=True, axis_index_groups=groups
        )

    def exchange(value):
        return lax.all_to_all(value, "expert", split_axis=0, concat_axis=0, tiled=True)

    token_rows = swap(tokens).reshape(row_count, model_width).astype(wide)

    choice_ids = routes.reshape(seq_dev, row_len * TOP)
    onehot = choice_ids[..., None] == jnp.arange(expert_total, dtype=jnp.int32)
    before_me = jnp.tri(row_len * TOP, k=-1, dtype=low)
    earlier = jnp.einsum("pq,sqe->spe", before_me, onehot.astype(low), preferred_element_type=wide)
    slot_index = jnp.sum(jnp.where(onehot, earlier, 0.0), axis=-1).astype(jnp.int32)
    place = choice_ids * capacity + slot_index
    home_code = jnp.where(keep_mask.reshape(choice_ids.shape) > 0, place, -1 - choice_ids)
    home_code = home_code.reshape(seq_dev, row_len, TOP)
    code = swap(home_code)

    def hits_of(codes):
        return [
            codes[:, :, k, None] == jnp.arange(slots, dtype=jnp.int32) for k in range(TOP)
        ]

    home_hits = hits_of(home_code)
    home_select = functools.reduce(jnp.logical_or, home_hits).astype(low)
    home_select = home_select.reshape(seq_dev, row_len, expert_total, capacity)
    cot_slots = jnp.einsum(
        "stec,std->escd", home_select, cotangent, preferred_element_type=wide
    ).astype(low)
    cot_rows = exchange(cot_slots)
    cot_rows = jnp.swapaxes(
        cot_rows.reshape(parts, seq_dev, seq_dev, capacity, model_width), 1, 2
    ).reshape(-1, model_width)
    grad_final = swap(cotangent).reshape(row_count, model_width).astype(wide)

    normal_one, spread_one = norm_parts(token_rows)
    low_one = (normal_one * norm_gain[0] + norm_bias[0]).astype(low)
    projected = jnp.dot(low_one, w_project, preferred_element_type=wide).astype(low)
    start = ((my_index // seq_dev) * row_count).astype(jnp.int32).reshape(1)
    pairs = HEADS // 2
    if whole:
        key_value, firsts = projected, (0, pairs, 2 * pairs)
    else:
        key_value = lax.all_gather(
            projected[:, model_width:], "expert", axis=0, tiled=True, axis_index_groups=across
        )
        firsts = (0, 0, pairs)
    attended_low, logs = attend(start, projected, key_value, key_value, firsts, whole)
    middle = token_rows + jnp.dot(attended_low, w_output, preferred_element_type=wide)
    normal_two, spread_two = norm_parts(middle)
    low_two = (normal_two * norm_gain[1] + norm_bias[1]).astype(low)

    hits = hits_of(code)
    select = functools.reduce(jnp.logical_or, hits).astype(low)
    select = select.reshape(seq_dev, row_len, expert_total, capacity)
    sending = jnp.einsum(
        "jtec,jtd->ejcd",
        select,
        low_two.reshape(seq_dev, row_len, model_width),
        preferred_element_type=wide,
    ).astype(low)
    received = exchange(sending).reshape(-1, model_width)

    low_two_wide = low_two.astype(wide)
    logits = jnp.dot(low_two_wide, router, precision=precise).reshape(
        seq_dev, row_len, 1, expert_total
    )
    route = jnp.where(code >= 0, code // capacity, -1 - code)
    onehot_four = (route[..., None] == jnp.arange(expert_total, dtype=jnp.int32)).astype(wide)
    gates = jax.nn.softmax(jnp.sum(onehot_four * logits, axis=-1), axis=-1)
    gate_slots = sum(
        jnp.sum(jnp.where(hits[k], gates[:, :, k, None], 0.0), axis=1) for k in range(TOP)
    )
    gate_slots = jnp.swapaxes(gate_slots.reshape(seq_dev, expert_total, capacity), 0, 1)
    gate_rows = exchange(gate_slots).reshape(-1, 1)

    w_first = expert_weights[0, 0]
    w_second = expert_weights[0, 1]
    before = jnp.dot(received, w_first, preferred_element_type=wide)
    activated, gelu_back = jax.vjp(jax.nn.gelu, before)
    pulled = jnp.dot(cot_rows, w_second, preferred_element_type=wide)
    gate_grad = jnp.sum(activated * pulled, axis=-1)
    grad_before = gelu_back(gate_rows * pulled)[0].astype(low)
    activated_low = activated.astype(low)
    grad_inputs = jnp.einsum("rf,df->rd", grad_before, w_first, preferred_element_type=wide).astype(
        low
    )
    slot_shape = (expert_count, seq_dev, capacity)
    grad_home = exchange(grad_inputs.reshape(slot_shape + (model_width,)))
    gate_grad_home = exchange(gate_grad.reshape(slot_shape))
    result = (
        jnp.einsum("rf,df->rd", activated_low, w_second, preferred_element_type=wide) * gate_rows
    ).astype(low)
    coming_back = exchange(result.reshape(slot_shape + (model_width,)))
    grad_flat = (gate_rows * cot_rows.astype(wide)).astype(low)
    grad_first_w = jnp.einsum("rd,rf->df", received, grad_before, preferred_element_type=wide)
    grad_second_w = jnp.einsum("rd,rf->df", grad_flat, activated_low, preferred_element_type=wide)
    flag_value = jnp.sum(
        frozen * (jnp.arange(frozen.shape[0], dtype=jnp.int32) == my_index).astype(jnp.int32)
    )
    trainable = (1 - flag_value).astype(wide)
    expert_stack = jnp.stack([grad_first_w, grad_second_w]) * trainable
    expert_grad = lax.psum_scatter(
        expert_stack.astype(low), "dp", scatter_dimension=2, tiled=True
    ).astype(wide)

    gate_grad_flat = jnp.swapaxes(gate_grad_home, 0, 1).reshape(seq_dev, 1, slots)
    grad_gate = jnp.stack(
        [jnp.sum(jnp.where(hits[k], gate_grad_flat, 0.0), axis=-1) for k in range(TOP)], axis=-1
    )
    grad_chosen = gates * (grad_gate - jnp.sum(gates * grad_gate, axis=-1, keepdims=True))
    grad_logits = jnp.sum(onehot_four * grad_chosen[..., None], axis=2).reshape(
        row_count, expert_total
    )
    router_local = jnp.dot(low_two_wide.T, grad_logits, precision=precise)
    grad_low_two = jnp.dot(grad_logits, router.T, precision=precise) + jnp.einsum(
        "jtec,ejcd->jtd", select, grad_home, preferred_element_type=wide
    ).reshape(row_count, model_width)
    moved_two, gain_two, bias_two = norm_back(grad_low_two, normal_two, spread_two, norm_gain[1])
    grad_middle = grad_final + moved_two
    grad_branch = grad_middle.astype(low)
    grad_w_output = jnp.einsum("rd,re->de", attended_low, grad_branch, preferred_element_type=wide)
    grad_attended = jnp.einsum("re,de->rd", grad_branch, w_output, preferred_element_type=wide).astype(
        low
    )

    mixture = jnp.einsum("jtec,ejcd->jtd", select, coming_back, preferred_element_type=wide)
    output = swap(
        (middle + mixture.reshape(row_count, model_width))
        .astype(low)
        .reshape(seq_dev, row_len, model_width)
    )

    grad_query, grad_keys, grad_values = attend_back(
        start, projected, key_value, key_value, firsts, grad_attended, attended_low, logs, whole
    )
    if not whole:
        grad_keys, grad_values = (
            lax.psum_scatter(
                g, "expert", scatter_dimension=0, tiled=True, axis_index_groups=across
            )
            for g in (grad_keys, grad_values)
        )
    grad_projected = jnp.concatenate([grad_query, grad_keys, grad_values], axis=1)
    grad_low_one = jnp.einsum("re,de->rd", grad_projected, w_project, preferred_element_type=wide)
    moved_one, gain_one, bias_one = norm_back(grad_low_one, normal_one, spread_one, norm_gain[0])
    input_grad = swap(
        (grad_middle + moved_one).astype(low).reshape(seq_dev, row_len, model_width)
    )

    grad_w_project = jnp.einsum("rd,re->de", low_one, grad_projected, preferred_element_type=wide)
    grad_norms = jnp.stack([gain_one, gain_two, bias_one, bias_two])
    block_width = attend_master.shape[2]
    grad_full = jnp.concatenate([grad_w_project, grad_w_output], axis=1).astype(low)
    slot_range = jnp.arange(expert_count, dtype=jnp.int32)
    which_block = jnp.sum(
        slot_range[None, :] * (owner_list[None, :] == slot_range[:, None]).astype(jnp.int32), axis=1
    )
    small = jnp.concatenate([router_local.reshape(-1), grad_norms.reshape(-1)])
    small_rows = small.shape[0] // block_width
    padded_rows = -(-small_rows // (16 * dp_count)) * 16 * dp_count
    small = jnp.pad(
        small.astype(low).reshape(small_rows, block_width), ((0, padded_rows - small_rows), (0, 0))
    )
    to_owner = jnp.stack(
        [
            jnp.concatenate(
                [
                    lax.dynamic_slice_in_dim(
                        grad_full, which_block[s] * block_width, block_width, 1
                    ),
                    small,
                ]
            )
            for s in range(expert_count)
        ]
    )
    my_rows = lax.psum_scatter(to_owner, "dp", scatter_dimension=1, tiled=True)
    my_rows = jnp.sum(exchange(my_rows).astype(wide), axis=0)
    summed = lax.all_gather(my_rows, "dp", axis=0, tiled=True)
    block_grad = summed[:model_width]
    small_sum = summed[model_width : model_width + small_rows].reshape(-1)
    router_grad = small_sum[: router.size].reshape(router.shape)
    norm_grad = small_sum[router.size :].reshape(grad_norms.shape)

    left_basis = attend_left[0].astype(low)
    right_basis = attend_right[0].astype(low)
    rotated = dot_low(dot_low(left_basis, block_grad, COL_COL), right_basis, ROW_COL)
    attend_first_new, attend_second_new, direction = adam_move(
        rotated, attend_first[0], attend_second[0]
    )
    stepped = dot_low(dot_low(left_basis, direction, ROW_COL), right_basis, ROW_ROW)
    attend_master_new = attend_master[0] - matrix_rate * stepped

    basis = expert_basis[0].astype(low)
    is_frozen = flag_value > 0
    news = []
    for i in range(2):
        rotated_one = dot_low(basis, expert_grad[i], COL_COL)
        first_new, second_new, move = adam_move(rotated_one, expert_first[0, i], expert_second[0, i])
        master_new = expert_master[0, i] - matrix_rate * dot_low(basis, move, ROW_COL)
        master_new = jnp.where(is_frozen, expert_master[0, i], master_new)
        news.append(
            (
                master_new,
                jnp.where(is_frozen, expert_first[0, i], first_new),
                jnp.where(is_frozen, expert_second[0, i], second_new),
                average_keep * expert_average[0, i] + (1.0 - average_keep) * master_new,
            )
        )
    expert_master_new, expert_first_new, expert_second_new, expert_average_new = (
        jnp.stack(pair) for pair in zip(*news)
    )

    router_first_new, router_second_new, router_step = adam_move(
        router_grad, router_first, router_second
    )
    router_new = router - matrix_rate * router_step
    norm_params = jnp.concatenate([norm_gain, norm_bias], axis=0)
    norm_first_new, norm_second_new, norm_step = adam_move(norm_grad, norm_first, norm_second)
    norm_new = norm_params - small_rate * norm_step
    return (
        output,
        input_grad,
        norm_grad,
        norm_new,
        norm_first_new,
        norm_second_new,
        router_grad,
        router_new,
        router_first_new,
        router_second_new,
        block_grad[None],
        attend_master_new[None],
        attend_first_new[None],
        attend_second_new[None],
        expert_grad[None],
        expert_master_new[None],
        expert_first_new[None],
        expert_second_new[None],
        expert_average_new[None],
    )


def solution(mesh):
    return jax.shard_map(
        on_device,
        mesh=mesh,
        in_specs=(
            P("dp", "expert", None),
            P("dp", "expert", None),
            P(),
            P(),
            P(),
            P(),
            P(),
            P("expert", None, None, None),
            P("dp", "expert", None),
            P("dp", "expert", None),
            P(),
            P(),
            P("expert", None, None),
            P("expert", None, None),
            P("expert", None, None),
            P("expert", None, None),
            P("expert", None, None),
            P("expert", None, None, "dp"),
            P("expert", None, None, "dp"),
            P("expert", None, None, "dp"),
            P("expert", None, None, "dp"),
            P("expert", None, None),
            P(),
            P(),
            P(),
            P(),
        ),
        out_specs=(
            P("dp", "expert", None),
            P("dp", "expert", None),
            P(),
            P(),
            P(),
            P(),
            P(),
            P(),
            P(),
            P(),
            P("expert", None, None),
            P("expert", None, None),
            P("expert", None, None),
            P("expert", None, None),
            P("expert", None, None, "dp"),
            P("expert", None, None, "dp"),
            P("expert", None, None, "dp"),
            P("expert", None, None, "dp"),
            P("expert", None, None, "dp"),
        ),
        check_vma=False,
    )
```

time: 1850 us -> 971 us (0.52)
  waiting for transfers between devices: 1070 us -> 271 us
  matrix products: 377 us -> 210 us
  blocking collectives: 41.3 us -> 116 us
  local copies, waits for them, and re-layouts: 191 us -> 120 us
  Pallas kernels: 0 us -> 60.2 us
  starting transfers between devices: 19.1 us -> 42.2 us
    all_gather x1, waiting for transfers between devices: 448 us -> 0.01 us  [on_device(): summed = lax.all_gather(my_rows, 'dp', axis=0, tiled=True)]
    reduce_scatter x2, waiting for transfers between devices: 336 us -> 0.02 us  [the longest x1 0.02 us: on_device(): lax.psum_scatter(expert_stack.astype(low), 'dp', scatter_dimension=2, til...]
    dot_general x26 -> x21, matrix products: 343 us -> 173 us  [the longest x1 33.3 us: on_device(): pulled = jnp.dot(cot_rows, w_second, preferred_element_type=wide)]
    all_to_all x0 -> x3, blocking collectives: none -> 116 us  [the longest x2 103 us: exchange(): lax.all_to_all(value, 'expert', split_axis=0, concat_axis=0, tiled=True)]
    psum x1 -> x0, waiting for transfers between devices: 70.7 us -> none  [on_device(): lax.psum((grad_attend_full, router_local, grad_norms), ('dp', 'expert'))]
    pallas_call x0 -> x2, Pallas kernels: none -> 60.2 us  [the longest x1 38.2 us: attend_back(): pl.pallas_call(functools.partial(attend_back_kernel, whole), grid=(pairs,...]
    all_to_all x4 -> x9, waiting for transfers between devices: 214 us -> 271 us  [the longest x5 201 us: exchange(): lax.all_to_all(value, 'expert', split_axis=0, concat_axis=0, tiled=True)]
    psum x1 -> x0, blocking collectives: 41.3 us -> none  [on_device(): lax.psum((grad_attend_full, router_local, grad_norms), ('dp', 'expert'))]
  transfers between devices with their start and end apart: 8 -> 12, of which waited for: 7 -> 8; matrix products, arithmetic and copies ran while one was open for 25% -> 26% of each run, Pallas kernels for 0% -> 2%
where the time goes in v1:
time: 971 us; the launch traced here: 965 us
  waiting for transfers between devices  271 us (28%)
  matrix products  210 us (22%)
  other arithmetic  123 us (13%)
  local copies, waits for them, and re-layouts  120 us (12%)
  blocking collectives  116 us (12%)
  Pallas kernels  60.2 us (6%)
  starting transfers between devices  42.2 us (4%)
  between operations  21.7 us (2%)
    all_to_all x5, waiting for transfers between devices, exchange(): lax.all_to_all(value, 'expert', split_axis=0, concat_axis=0, tiled=True)  201 us
    all_to_all x2, blocking collectives, exchange(): lax.all_to_all(value, 'expert', split_axis=0, concat_axis=0, tiled=True)  103 us
    unnamed x178, local copies, waits for them, and re-layouts  70.7 us
    all_to_all x4, waiting for transfers between devices, swap(): lax.all_to_all(value, 'expert', split_axis=0, concat_axis=0, tiled=True,...  70.2 us
    pallas_call x1, Pallas kernels, attend_back(): pl.pallas_call(functools.partial(attend_back_kernel, whole), grid=(pairs,...  38.2 us
    dot_general x1, matrix products, on_device(): pulled = jnp.dot(cot_rows, w_second, preferred_element_type=wide)  33.3 us
    convert_element_type x1, other arithmetic, on_device(): grad_before = gelu_back(gate_rows * pulled)[0].astype(low)  32 us
    dot_general x1, matrix products, on_device(): jnp.einsum('rf,df->rd', activated_low, w_second, preferred_element_type=w...  25.3 us
  transfers between devices with their start and end apart: 12, of which 8 were waited for; matrix products, arithmetic and copies ran while one was open for 26% of the time, Pallas kernels for 2%

profile of v1, /device:TPU:0, one launch (start us, length us, event | category | flops | bytes accessed | tf_op | source)
XLA Modules:
  0.0 965.0 jit_solution(737113153744454694)
XLA Ops:
  13.2 13.7 %all_to_all.60 = s32[8,128,2]{1,2,0:T(2,128)} all-to-all(s32[8,128,2]{1,2,0:T(2,128)S(1)} %copy.337), channel_id=1, replica_groups=mesh['dp'=4,'expert'=8] {'expert'}, dimensions={0} | all-to-all | bytes 16384 | tf_op jit(solution)/shard_map/all_to_all | solution.py:259
  27.0 4.3 all-to-all-start
  36.1 31.1 %all-to-all-done = bf16[8,128,768]{2,1,0:T(8,128)(2,1)} async-done(((bf16[8,128,768]{2,1,0:T(8,128)(2,1)}), bf16[8,128,768]{2,1,0:T(8,128)(2,1)}, u32[]{:S(2)}, u32[]{:S(2)}) %all-to-all-start) | async-done | bytes 1572896 | tf_op jit(solution)/shard_map/all_to_all | solution.py:259
  67.3 4.7 all-to-all-start.7
  81.6 5.5 convolution_convert_fusion.q_ref.k_ref.v_ref
  87.1 22.0 %attend.1 = (bf16[1024,768]{1,0:T(8,128)(2,1)}, f32[1024,768]{1,0:T(8,128)}) custom-call(s32[1]{0:T(128)} %bitcast.1.start_ref, bf16[1024,2304]{1,0:T(8,128)(2,1)} %convolution_convert_fusion.q_ref.k_ref.v_ref, bf16[1024,2304]{1,0:T(8,128)(2,1)} %convolution_convert_fusion.q_ref.k_ref.v_ref, bf16[1024,2304]{1,0:T(8,128)(2,1)} %convolution_convert_fusion.q_ref.k_ref.v_ref), custom_call_target="tpu_custom_call" | custom-call | flops 1610612736 | bytes 9437184 | tf_op jit(solution)/shard_map/attend/pallas_call | solution.py:161
  109.0 3.8 fusion.193
  118.6 40.2 %all-to-all-done.7 = bf16[8,8,40,768]{3,2,1,0:T(8,128)(2,1)} async-done(((bf16[8,8,40,768]{3,2,1,0:T(8,128)(2,1)}), bf16[8,8,40,768]{3,2,1,0:T(8,128)(2,1)}, u32[]{:S(2)}, u32[]{:S(2)}) %all-to-all-start.7) | async-done | bytes 3932192 | tf_op jit(solution)/shard_map/all_to_all | solution.py:264
  158.7 4.8 all-to-all-start.2
  167.0 4.3 copy.350
  171.3 79.1 %all-to-all-done.2 = bf16[8,8,40,768]{3,2,1,0:T(8,128)(2,1)} async-done(((bf16[8,8,40,768]{3,2,1,0:T(8,128)(2,1)}), bf16[8,8,40,768]{3,2,1,0:T(8,128)(2,1)}, u32[]{:S(2)}, u32[]{:S(2)}) %all-to-all-start.2) | async-done | bytes 3932192 | tf_op jit(solution)/shard_map/all_to_all | solution.py:264
  250.5 21.0 %fusion.14 = f32[2560,3072]{1,0:T(8,128)} fusion(bf16[2560,768]{1,0:T(8,128)(2,1)} %bitcast.14, bf16[1,2,768,3072]{3,2,1,0:T(8,128)(2,1)} %param.33), kind=kOutput, calls=%fused_computation.46 | convolution fusion | flops 12079595520 | bytes 40108032 | tf_op jit(solution)/shard_map/dot_general | solution.py:338
  271.4 33.3 %multiply_reduce_fusion = (f32[2560]{0:T(1024)}, f32[2560,3072]{1,0:T(8,128)}) fusion(f32[2560,3072]{1,0:T(8,128)} %fusion.14, bf16[2560,768]{1,0:T(8,128)(2,1)} %bitcast.357, bf16[1,2,768,3072]{3,2,1,0:T(8,128)(2,1)} %param.33), kind=kOutput, calls=%fused_computation.10 | convolution fusion | flops 12158236672 | bytes 71575552 | tf_op jit(solution)/shard_map/dot_general | solution.py:340
  307.6 4.0 all-to-all-start.8
  312.2 6.0 all-to-all-done.8
  332.4 11.0 %all_to_all.61 = f32[8,1,320]{2,1,0:T(1,128)} all-to-all(f32[8,1,320]{2,1,0:T(1,128)} %reshape.278), channel_id=1, replica_groups=mesh['dp'=4,'expert'=8] {'expert'}, dimensions={0} | all-to-all | bytes 20480 | tf_op jit(solution)/shard_map/all_to_all | solution.py:264
  348.2 32.0 %fusion.7 = bf16[2560,3072]{1,0:T(8,128)(2,1)} fusion(f32[2560,3072]{1,0:T(8,128)} %fusion.14, f32[2560,3072]{1,0:T(8,128)} %get-tuple-element.227, f32[2560]{0:T(1024)} %mul.444), kind=kLoop, calls=%fused_computation.9 | loop fusion | flops 165150720 | bytes 78653440 | tf_op jit(solution)/shard_map/convert_element_type | solution.py:342
  380.2 17.8 %convolution_convert_fusion.2 = bf16[2560,768]{1,0:T(8,128)(2,1)} fusion(bf16[2560,3072]{1,0:T(8,128)(2,1)} %fusion.7, bf16[1,2,768,3072]{3,2,1,0:T(8,128)(2,1)} %param.33), kind=kOutput, calls=%fused_computation.29 | convolution fusion | flops 12081561600 | bytes 24379392 | tf_op jit(solution)/shard_map/rf,df->rd/dot_general | solution.py:344
  398.1 4.7 all-to-all-start.9
  402.8 25.3 %multiply_convert_fusion.1 = bf16[2560,768]{1,0:T(8,128)(2,1)} fusion(bf16[1,2,768,3072]{3,2,1,0:T(8,128)(2,1)} %param.33, f32[2560]{0:T(1024)} %mul.444, f32[2560,3072]{1,0:T(8,128)} %fusion.14), kind=kOutput, calls=%fused_computation.24 | convolution fusion | flops 12154306560 | bytes 40120320 | tf_op jit(solution)/shard_map/rf,df->rd/dot_general | solution.py:351
  428.0 59.9 %all-to-all-done.9 = bf16[8,8,40,768]{3,2,1,0:T(8,128)(2,1)} async-done(((bf16[8,8,40,768]{3,2,1,0:T(8,128)(2,1)}), bf16[8,8,40,768]{3,2,1,0:T(8,128)(2,1)}, u32[]{:S(2)}, u32[]{:S(2)}) %all-to-all-start.9) | async-done | bytes 3932192 | tf_op jit(solution)/shard_map/all_to_all | solution.py:264
  488.0 91.7 %all_to_all.62 = bf16[8,8,40,768]{3,2,1,0:T(8,128)(2,1)} all-to-all(bf16[8,8,40,768]{3,2,1,0:T(8,128)(2,1)} %bitcast.360), channel_id=1, replica_groups=mesh['dp'=4,'expert'=8] {'expert'}, dimensions={0} | all-to-all | bytes 7864320 | tf_op jit(solution)/shard_map/all_to_all | solution.py:264
  579.6 4.4 all-to-all-start.6
  599.8 3.4 fusion.20
  603.3 6.1 multiply_reduce_fusion.1
  610.0 2.8 fusion.22
  612.8 7.3 all-to-all-done.6
  620.2 6.2 convert_add_fusion
  631.4 38.2 %attend_back.1 = (bf16[1024,768]{1,0:T(8,128)(2,1)}, bf16[1024,768]{1,0:T(8,128)(2,1)}, bf16[1024,768]{1,0:T(8,128)(2,1)}) custom-call(s32[1]{0:T(128)} %bitcast.1.start_ref, bf16[1024,2304]{1,0:T(8,128)(2,1)} %convolution_convert_fusion.q_ref.k_ref.v_ref, bf16[1024,2304]{1,0:T(8,128)(2,1)} %convolution_convert_fusion.q_ref.k_ref.v_ref, ...), custom_call_target="tpu_custom_call" | custom-call | flops 4026531840 | bytes 15728640 | tf_op jit(solution)/shard_map/attend_back/pallas_call | solution.py:186
  673.2 5.4 convolution_convert_fusion.1
  678.7 7.5 fusion.40
  686.4 3.3 fusion.116
  701.0 19.4 %convolution_bitcast_fusion.1 = f32[1,768,3072]{2,1,0:T(8,128)} fusion(bf16[2560,768]{1,0:T(8,128)(2,1)} %bitcast.14, bf16[2560,3072]{1,0:T(8,128)(2,1)} %fusion.7), kind=kOutput, calls=%fused_computation.27 | convolution fusion | flops 12079595520 | bytes 29097984 | tf_op jit(solution)/shard_map/rd,rf->df/dot_general | solution.py:355
  720.4 23.1 %convolution_bitcast_fusion = f32[1,768,3072]{2,1,0:T(8,128)} fusion(bf16[2560,768]{1,0:T(8,128)(2,1)} %bitcast.358, f32[2560]{0:T(1024)S(1)} %copy-done.52, f32[2560,3072]{1,0:T(8,128)} %fusion.14), kind=kOutput, calls=%fused_computation.26 | convolution fusion | flops 12156272640 | bytes 44836864 | tf_op jit(solution)/shard_map/rd,rf->df/dot_general | solution.py:356
  743.5 11.7 %fusion.8 = bf16[2,768,3072]{2,1,0:T(8,128)(2,1)} fusion(f32[1,768,3072]{2,1,0:T(8,128)} %convolution_bitcast_fusion, f32[1,768,3072]{2,1,0:T(8,128)} %convolution_bitcast_fusion.1, f32[]{:T(128)S(6)} %convert_element_type.182), kind=kLoop, calls=%fused_computation.13 | loop fusion | flops 14155776 | bytes 28311556 | tf_op jit(solution)/shard_map/convert_element_type | solution.py:363
  755.3 4.8 all-to-all-start.5
  760.2 4.5 fusion.39
  764.7 31.7 %all-to-all-done.5 = bf16[8,128,768]{2,1,0:T(8,128)(2,1)} async-done(((bf16[8,128,768]{2,1,0:T(8,128)(2,1)}), bf16[8,128,768]{2,1,0:T(8,128)(2,1)}, u32[]{:S(2)}, u32[]{:S(2)}) %all-to-all-start.5) | async-done | bytes 1572896 | tf_op jit(solution)/shard_map/all_to_all | solution.py:259
  796.4 4.3 all-to-all-start.10
  801.3 4.1 fusion.189
  809.2 4.9 fusion.188
  816.1 4.9 fusion.187
  821.0 3.1 copy.386
  824.0 3.1 copy.381
  827.1 3.0 copy.382
  830.1 3.0 copy.383
  833.2 4.9 fusion.186
  838.0 3.1 copy.388
  841.1 3.0 copy.387
  844.2 5.9 all-to-all-start.11
  856.0 3.9 subtract_select_fusion
  860.8 3.9 subtract_select_fusion.1
  864.6 15.5 %all-to-all-done.11 = bf16[8,208,384]{2,1,0:T(8,128)(2,1)} async-done(((bf16[8,208,384]{2,1,0:T(8,128)(2,1)}), bf16[8,208,384]{2,1,0:T(8,128)(2,1)}, u32[]{:S(2)}, u32[]{:S(2)}) %all-to-all-start.11) | async-done | bytes 1277984 | tf_op jit(solution)/shard_map/all_to_all | solution.py:264
  882.4 9.0 fusion.45
  893.9 6.4 copy.370
  900.3 4.2 maximum_bitcast_fusion.1
  904.5 6.2 copy.371
  910.7 4.2 maximum_bitcast_fusion.2
  914.9 6.2 copy.372
  921.1 3.9 fusion.43
  927.4 6.2 copy.373
  938.6 3.8 fusion.58
  944.2 5.9 fusion.53
  952.6 2.8 copy.409
  (270 shorter events, 114.0 us)
Async XLA Ops:
  7.2 74.4 %copy-start = (bf16[768,2304]{1,0:T(8,128)(2,1)S(1)}, bf16[768,2304]{1,0:T(8,128)(2,1)}, u32[]{:S(2)}) copy-start(bf16[768,2304]{1,0:T(8,128)(2,1)} %param.28) | copy-start | bytes 10616836
  27.0 40.3 %all-to-all-start = ((bf16[8,128,768]{2,1,0:T(8,128)(2,1)}), bf16[8,128,768]{2,1,0:T(8,128)(2,1)}, u32[]{:S(2)}, u32[]{:S(2)}) async-start(bf16[8,128,768]{2,1,0:T(8,128)(2,1)} %param.26), calls=%async_computation | async-start | bytes 3145728 | tf_op jit(solution)/shard_map/all_to_all | solution.py:259
  31.3 43.0 %copy-start.38 = (s32[8,40]{1,0:T(8,128)}, s32[8,40]{1,0:T(8,128)S(1)}, u32[]{:S(2)}) copy-start(s32[8,40]{1,0:T(8,128)S(1)} %multiply_add_fusion.2) | copy-start | bytes 3844
  36.1 35.9 %copy-start.65 = (f32[2,768]{1,0:T(2,128)S(1)}, f32[2,768]{1,0:T(2,128)}, u32[]{:S(2)}) copy-start(f32[2,768]{1,0:T(2,128)} %param.31) | copy-start | bytes 18436
  67.3 91.5 %all-to-all-start.7 = ((bf16[8,8,40,768]{3,2,1,0:T(8,128)(2,1)}), bf16[8,8,40,768]{3,2,1,0:T(8,128)(2,1)}, u32[]{:S(2)}, u32[]{:S(2)}) async-start(bf16[8,8,40,768]{3,2,1,0:T(8,128)(2,1)} %copy.349), calls=%async_computation.7 | async-start | bytes 7864320 | tf_op jit(solution)/shard_map/all_to_all | solution.py:264
  73.4 5.5 copy-start.53
  73.4 40.0 %copy-start.46 = (f32[768]{0:T(1024)}, f32[768]{0:T(1024)S(1)}, u32[]{:S(2)}) copy-start(f32[768]{0:T(1024)S(1)} %get-tuple-element.172) | copy-start | bytes 9220
  81.6 5.5 copy-start.25
  118.6 45.0 %copy-start.44 = (s32[8,128,2]{1,2,0:T(2,128)S(1)}, s32[8,128,2]{1,2,0:T(2,128)}, u32[]{:S(2)}) copy-start(s32[8,128,2]{1,2,0:T(2,128)} %all_to_all.60) | copy-start | bytes 24580
  158.7 91.7 %all-to-all-start.2 = ((bf16[8,8,40,768]{3,2,1,0:T(8,128)(2,1)}), bf16[8,8,40,768]{3,2,1,0:T(8,128)(2,1)}, u32[]{:S(2)}, u32[]{:S(2)}) async-start(bf16[8,8,40,768]{3,2,1,0:T(8,128)(2,1)} %copy.338), calls=%async_computation.2 | async-start | bytes 7864320 | tf_op jit(solution)/shard_map/all_to_all | solution.py:264
  163.6 3.4 copy-start.45
  307.6 10.5 %all-to-all-start.8 = ((f32[8,1,320]{2,1,0:T(1,128)}), f32[8,1,320]{2,1,0:T(1,128)}, u32[]{:S(2)}, u32[]{:S(2)}) async-start(f32[8,1,320]{2,1,0:T(1,128)} %reshape.276), calls=%async_computation.8 | async-start | bytes 24576 | tf_op jit(solution)/shard_map/all_to_all | solution.py:264
  398.1 89.9 %all-to-all-start.9 = ((bf16[8,8,40,768]{3,2,1,0:T(8,128)(2,1)}), bf16[8,8,40,768]{3,2,1,0:T(8,128)(2,1)}, u32[]{:S(2)}, u32[]{:S(2)}) async-start(bf16[8,8,40,768]{3,2,1,0:T(8,128)(2,1)} %bitcast.359), calls=%async_computation.9 | async-start | bytes 7864320 | tf_op jit(solution)/shard_map/all_to_all | solution.py:264
  579.6 11.3 %copy-start.62 = (f32[8,128]{1,0:T(8,128)S(1)}, f32[8,128]{1,0:T(8,128)}, u32[]{:S(2)}) copy-start(f32[8,128]{1,0:T(8,128)} %copy-done.61) | copy-start | bytes 12292
  579.6 20.2 %copy-start.39 = (s32[8,40]{1,0:T(8,128)S(1)}, s32[8,40]{1,0:T(8,128)}, u32[]{:S(2)}) copy-start(s32[8,40]{1,0:T(8,128)} %copy-done.38) | copy-start | bytes 3844
  579.6 40.5 %all-to-all-start.6 = ((bf16[8,128,768]{2,1,0:T(8,128)(2,1)}), bf16[8,128,768]{2,1,0:T(8,128)(2,1)}, u32[]{:S(2)}, u32[]{:S(2)}) async-start(bf16[8,128,768]{2,1,0:T(8,128)(2,1)} %param.27), calls=%async_computation.6 | async-start | bytes 3145728 | tf_op jit(solution)/shard_map/all_to_all | solution.py:259
  584.1 260.1 %reduce-scatter.3.cloned.1.call-start = ((), (), s32[]{:S(2)}) async-start(), calls=%async_computation.14 | async-start | bytes 6389760 | tf_op jit(solution)/shard_map/reduce_scatter | solution.py:437
  599.8 3.4 copy-start.36
  599.8 3.4 copy-start.41
  599.8 3.4 copy-start.47
  599.8 3.4 copy-start.49
  603.3 6.7 copy-start.5
  620.2 6.2 copy-start.75
  673.2 5.4 copy-start.54
  673.2 5.4 copy-start.56
  673.2 5.4 copy-start.59
  678.7 7.6 copy-start.71
  678.7 7.6 copy-start.50
  690.6 5.2 copy-start.6
  690.6 5.2 copy-start.17
  699.1 151.1 %reduce-scatter.5.cloned.1.call-start = ((), (), s32[]{:S(2)}) async-start(), calls=%async_computation.16 | async-start | bytes 11796480 | tf_op jit(solution)/shard_map/reduce_scatter | solution.py:362
  701.0 19.4 %copy-start.52 = (f32[2560]{0:T(1024)S(1)}, f32[2560]{0:T(1024)}, u32[]{:S(2)}) copy-start(f32[2560]{0:T(1024)} %mul.444) | copy-start | bytes 30724
  755.3 4.9 copy-start.74
  755.3 4.9 copy-start.73
  755.3 4.9 copy-start.8
  755.3 4.9 copy-start.57
  755.3 4.9 copy-start.60
  755.3 41.1 %all-to-all-start.5 = ((bf16[8,128,768]{2,1,0:T(8,128)(2,1)}), bf16[8,128,768]{2,1,0:T(8,128)(2,1)}, u32[]{:S(2)}, u32[]{:S(2)}) async-start(bf16[8,128,768]{2,1,0:T(8,128)(2,1)} %bitcast.355), calls=%async_computation.5 | async-start | bytes 3145728 | tf_op jit(solution)/shard_map/all_to_all | solution.py:259
  796.4 47.8 %all-to-all-start.10 = ((bf16[8,128,768]{2,1,0:T(8,128)(2,1)}), bf16[8,128,768]{2,1,0:T(8,128)(2,1)}, u32[]{:S(2)}, u32[]{:S(2)}) async-start(bf16[8,128,768]{2,1,0:T(8,128)(2,1)} %bitcast.356), calls=%async_computation.10 | async-start | bytes 3145728 | tf_op jit(solution)/shard_map/all_to_all | solution.py:259
  844.2 36.0 %all-to-all-start.11 = ((bf16[8,208,384]{2,1,0:T(8,128)(2,1)}), bf16[8,208,384]{2,1,0:T(8,128)(2,1)}, u32[]{:S(2)}, u32[]{:S(2)}) async-start(bf16[8,208,384]{2,1,0:T(8,128)(2,1)} %reduce-scatter.3.cloned.1.call-done), calls=%async_computation.12 | async-start | bytes 2555904 | tf_op jit(solution)/shard_map/all_to_all | solution.py:264
  850.1 86.1 %all-gather.2.cloned.1.call-start = ((), (), s32[]{:S(2)}) async-start(), calls=%async_computation.15 | async-start | bytes 1597440 | tf_op jit(solution)/shard_map/all_gather | solution.py:439
  856.0 3.9 copy-start.20
  856.0 3.9 copy-start.10
  856.0 3.9 copy-start.11
  856.0 4.8 copy-start.24
  882.4 9.0 copy-start.15
  882.4 9.0 copy-start.16
  893.9 6.4 copy-start.13
  904.5 6.2 copy-start.12
  914.9 6.2 copy-start.14
  927.4 6.2 copy-start.22
  936.9 13.3 %copy-start.51 = (f32[4,768]{1,0:T(4,128)}, f32[4,768]{1,0:T(4,128)S(1)}, u32[]{:S(2)}) copy-start(f32[4,768]{1,0:T(4,128)S(1)} %reshape.261) | copy-start | bytes 36868
  938.6 3.8 copy-start.32
  938.6 3.8 copy-start.33
  944.2 6.0 copy-start.66
  944.2 6.0 copy-start.67
  944.2 6.0 copy-start.69
  944.2 6.0 copy-start.70
  944.2 6.7 copy-start.37
  944.2 6.6 copy-start.42
  944.2 6.6 copy-start.63
  944.2 6.6 copy-start.64
  944.2 7.3 copy-start.18
  952.6 5.5 copy-start.1
  (26 other events, 48.0 us)
Sparse Core Ops, SparseCore 0:
  699.2 49.3 reduce-scatter.2
  755.4 76.3 reduce-scatter.4
  882.5 16.8 all-gather.1

commit v2 on v1

--- a/solution.py
+++ b/solution.py
@@ -11,6 +11,9 @@
 HEAD_DIM = 64
 TOP = 2
 TILE = 256
+CHUNK = 512
+ROOT = 0.7978845608028654
+CUBIC = 0.044715
 
 
 norm_epsilon = 1e-05
@@ -210,6 +213,160 @@
         ),
         name="attend_back",
     )(start, queries, keys, values, grads, attended, logs)
+
+
+def expert_kernel(x_ref, u_ref, gate_ref, w_ref, act_ref, grad_ref, input_ref, gate_grad_ref):
+    x, gate = x_ref[...], gate_ref[...]
+    inputs, gate_grad = None, None
+    hidden = w_ref.shape[1]
+    for first in range(0, hidden, CHUNK):
+        at = slice(first, first + CHUNK)
+        w = w_ref[:, at]
+        v = dot_low(x, w, ROW_COL)
+        u = u_ref[:, at].astype(wide)
+        square = v * v
+        t = jnp.tanh(ROOT * v * (1.0 + CUBIC * square))
+        half = 0.5 * (1.0 + t)
+        act = v * half
+        slope = half + 0.5 * ROOT * v * (1.0 - t * t) * (1.0 + 3.0 * CUBIC * square)
+        grad = (gate * u * slope).astype(low)
+        act_ref[:, at] = act.astype(low)
+        grad_ref[:, at] = grad
+        here = jnp.sum(act * u, axis=-1, keepdims=True)
+        add = dot_low(grad, w, ROW_ROW)
+        gate_grad = here if gate_grad is None else gate_grad + here
+        inputs = add if inputs is None else inputs + add
+    input_ref[...] = inputs.astype(low)
+    gate_grad_ref[...] = gate_grad
+
+
+def expert_stage(x, u, gate, w):
+    rows, width = x.shape
+    hidden = w.shape[1]
+
+    def row_block(columns):
+        return pl.BlockSpec((TILE, columns), lambda i: (i, 0))
+
+    return pl.pallas_call(
+        expert_kernel,
+        grid=(rows // TILE,),
+        out_shape=(
+            jax.ShapeDtypeStruct((rows, hidden), low),
+            jax.ShapeDtypeStruct((rows, hidden), low),
+            jax.ShapeDtypeStruct((rows, width), low),
+            jax.ShapeDtypeStruct((rows, 1), wide),
+        ),
+        in_specs=[
+            row_block(width),
+            row_block(hidden),
+            row_block(1),
+            pl.BlockSpec((width, hidden), lambda i: (0, 0)),
+        ],
+        out_specs=(row_block(hidden), row_block(hidden), row_block(width), row_block(1)),
+        cost_estimate=pl.CostEstimate(
+            flops=4 * rows * width * hidden,
+            bytes_accessed=6 * rows * hidden,
+            transcendentals=rows * hidden,
+        ),
+        name="expert_stage",
+    )(x, u, gate, w)
+
+
+def refresh_kernel(
+    flag_ref,
+    basis_ref,
+    turned_ref,
+    grad_ref,
+    master_ref,
+    first_ref,
+    second_ref,
+    average_ref,
+    grad_out,
+    master_out,
+    first_out,
+    second_out,
+    average_out,
+):
+    is_frozen = flag_ref[0] > 0
+    grad = grad_ref[0]
+    grad_out[0, 0] = grad.astype(wide)
+    first_new, second_new, move = adam_move(
+        dot_low(turned_ref[...], grad, ROW_COL), first_ref[0, 0], second_ref[0, 0]
+    )
+    master_new = master_ref[0, 0] - matrix_rate * dot_low(basis_ref[...], move, ROW_COL)
+    master_new = jnp.where(is_frozen, master_ref[0, 0], master_new)
+    master_out[0, 0] = master_new
+    first_out[0, 0] = jnp.where(is_frozen, first_ref[0, 0], first_new)
+    second_out[0, 0] = jnp.where(is_frozen, second_ref[0, 0], second_new)
+    average_out[0, 0] = average_keep * average_ref[0, 0] + (1.0 - average_keep) * master_new
+
+
+def refresh(flag, basis, grad, master, first, second, average):
+    _, mats, width, columns = master.shape
+    step = 256 if columns % 256 == 0 else 128
+    block = pl.BlockSpec((1, 1, width, step), lambda i, j: (0, i, 0, j))
+    square = pl.BlockSpec((width, width), lambda i, j: (0, 0))
+    return pl.pallas_call(
+        refresh_kernel,
+        grid=(mats, columns // step),
+        out_shape=(jax.ShapeDtypeStruct(master.shape, wide),) * 5,
+        in_specs=[
+            pl.BlockSpec(memory_space=pltpu.SMEM),
+            square,
+            square,
+            pl.BlockSpec((1, width, step), lambda i, j: (i, 0, j)),
+        ]
+        + [block] * 4,
+        out_specs=(block,) * 5,
+        cost_estimate=pl.CostEstimate(
+            flops=4 * mats * width * width * columns,
+            bytes_accessed=38 * mats * width * columns,
+            transcendentals=0,
+        ),
+        name="refresh",
+    )(flag, basis, basis.T, grad, master, first, second, average)
+
+
+def deal_kernel(which_ref, block_ref, small_ref, out_ref):
+    width = block_ref.shape[1]
+    out_ref[0, :, :width] = block_ref[...]
+    out_ref[0, :, width:] = small_ref[...]
+
+
+def deal(which, rows, block_width, count):
+    height, total = rows.shape
+    extra = total - block_width * count
+    if block_width % 128:
+        return jnp.stack(
+            [
+                jnp.concatenate(
+                    [
+                        lax.dynamic_slice_in_dim(rows, which[s] * block_width, block_width, 1),
+                        rows[:, total - extra :],
+                    ],
+                    axis=1,
+                )
+                for s in range(count)
+            ]
+        )
+    return pl.pallas_call(
+        deal_kernel,
+        grid_spec=pltpu.PrefetchScalarGridSpec(
+            num_scalar_prefetch=1,
+            grid=(count,),
+            in_specs=[
+                pl.BlockSpec((height, block_width), lambda s, which: (0, which[s])),
+                pl.BlockSpec((height, extra), lambda s, which: (0, total // extra - 1)),
+            ],
+            out_specs=pl.BlockSpec((1, height, block_width + extra), lambda s, which: (s, 0, 0)),
+        ),
+        out_shape=jax.ShapeDtypeStruct((count, height, block_width + extra), rows.dtype),
+        name="deal",
+    )(which, rows, rows)
+
+
+def after(value, *others):
+    return lax.optimization_barrier((value, *others))[0]
 
 
 def on_device(
@@ -260,10 +417,27 @@
             value, "expert", split_axis=0, concat_axis=0, tiled=True, axis_index_groups=groups
         )
 
+    def sum_dp(value):
+        lines = dp_count // 2
+        mine = lax.axis_index("dp")
+        line, core = mine // 2, mine % 2
+        cut = value.reshape(lines, 2, value.shape[0] // dp_count, value.shape[1])
+        given = lax.dynamic_index_in_dim(cut, 1 - core, 1, keepdims=False)
+        kept = lax.dynamic_index_in_dim(cut, core, 1, keepdims=False)
+        got = lax.ppermute(given, "dp", [(d, d ^ 1) for d in range(dp_count)])
+        half = (kept.astype(wide) + got.astype(wide)).astype(low)
+        total = lax.dynamic_index_in_dim(half, line, 0, keepdims=False).astype(wide)
+        for shift in range(1, lines):
+            given = lax.dynamic_index_in_dim(half, (line + shift) % lines, 0, keepdims=False)
+            moves = [(d, (d + 2 * shift) % dp_count) for d in range(dp_count)]
+            total = total + lax.ppermute(given, "dp", moves).astype(wide)
+        return total.astype(low)
+
     def exchange(value):
         return lax.all_to_all(value, "expert", split_axis=0, concat_axis=0, tiled=True)
 
-    token_rows = swap(tokens).reshape(row_count, model_width).astype(wide)
+    token_seq = swap(tokens)
+    token_rows = token_seq.reshape(row_count, model_width).astype(wide)
 
     choice_ids = routes.reshape(seq_dev, row_len * TOP)
     onehot = choice_ids[..., None] == jnp.arange(expert_total, dtype=jnp.int32)
@@ -272,12 +446,17 @@
     slot_index = jnp.sum(jnp.where(onehot, earlier, 0.0), axis=-1).astype(jnp.int32)
     place = choice_ids * capacity + slot_index
     home_code = jnp.where(keep_mask.reshape(choice_ids.shape) > 0, place, -1 - choice_ids)
-    home_code = home_code.reshape(seq_dev, row_len, TOP)
-    code = swap(home_code)
+    home_code = jnp.swapaxes(home_code.reshape(seq_dev, row_len, TOP), 1, 2)
+    all_codes = lax.all_gather(home_code, "expert", axis=0)
+    code = lax.dynamic_slice(
+        all_codes,
+        ((my_index // seq_dev) * seq_dev, my_index % seq_dev, 0, 0),
+        (seq_dev, 1, TOP, row_len),
+    )[:, 0]
 
     def hits_of(codes):
         return [
-            codes[:, :, k, None] == jnp.arange(slots, dtype=jnp.int32) for k in range(TOP)
+            codes[:, k, :, None] == jnp.arange(slots, dtype=jnp.int32) for k in range(TOP)
         ]
 
     home_hits = hits_of(home_code)
@@ -286,11 +465,10 @@
     cot_slots = jnp.einsum(
         "stec,std->escd", home_select, cotangent, preferred_element_type=wide
     ).astype(low)
-    cot_rows = exchange(cot_slots)
+    cot_back = exchange(after(cot_slots, token_seq))
     cot_rows = jnp.swapaxes(
-        cot_rows.reshape(parts, seq_dev, seq_dev, capacity, model_width), 1, 2
+        cot_back.reshape(parts, seq_dev, seq_dev, capacity, model_width), 1, 2
     ).reshape(-1, model_width)
-    grad_final = swap(cotangent).reshape(row_count, model_width).astype(wide)
 
     normal_one, spread_one = norm_parts(token_rows)
     low_one = (normal_one * norm_gain[0] + norm_bias[0]).astype(low)
@@ -318,39 +496,42 @@
         low_two.reshape(seq_dev, row_len, model_width),
         preferred_element_type=wide,
     ).astype(low)
-    received = exchange(sending).reshape(-1, model_width)
+    received = exchange(after(sending, cot_back))
+    cot_seq = swap(after(cotangent, received))
+    grad_final = cot_seq.reshape(row_count, model_width).astype(wide)
+    received = received.reshape(-1, model_width)
 
     low_two_wide = low_two.astype(wide)
     logits = jnp.dot(low_two_wide, router, precision=precise).reshape(
-        seq_dev, row_len, 1, expert_total
+        seq_dev, 1, row_len, expert_total
     )
     route = jnp.where(code >= 0, code // capacity, -1 - code)
     onehot_four = (route[..., None] == jnp.arange(expert_total, dtype=jnp.int32)).astype(wide)
-    gates = jax.nn.softmax(jnp.sum(onehot_four * logits, axis=-1), axis=-1)
+    gates = jax.nn.softmax(jnp.sum(onehot_four * logits, axis=-1), axis=1)
     gate_slots = sum(
-        jnp.sum(jnp.where(hits[k], gates[:, :, k, None], 0.0), axis=1) for k in range(TOP)
+        jnp.sum(jnp.where(hits[k], gates[:, k, :, None], 0.0), axis=1) for k in range(TOP)
     )
     gate_slots = jnp.swapaxes(gate_slots.reshape(seq_dev, expert_total, capacity), 0, 1)
-    gate_rows = exchange(gate_slots).reshape(-1, 1)
+    gate_slots = gate_slots.reshape(expert_total, seq_dev * capacity)
+    gate_rows = lax.all_gather(gate_slots, "expert", axis=0)
+    gate_rows = lax.dynamic_index_in_dim(gate_rows, my_index, 1, keepdims=False).reshape(-1, 1)
 
     w_first = expert_weights[0, 0]
     w_second = expert_weights[0, 1]
-    before = jnp.dot(received, w_first, preferred_element_type=wide)
-    activated, gelu_back = jax.vjp(jax.nn.gelu, before)
-    pulled = jnp.dot(cot_rows, w_second, preferred_element_type=wide)
-    gate_grad = jnp.sum(activated * pulled, axis=-1)
-    grad_before = gelu_back(gate_rows * pulled)[0].astype(low)
-    activated_low = activated.astype(low)
-    grad_inputs = jnp.einsum("rf,df->rd", grad_before, w_first, preferred_element_type=wide).astype(
-        low
+    pulled = jnp.dot(cot_rows, w_second, preferred_element_type=wide).astype(low)
+    activated_low, grad_before, grad_inputs, gate_grad = expert_stage(
+        received, pulled, gate_rows, w_first
     )
     slot_shape = (expert_count, seq_dev, capacity)
-    grad_home = exchange(grad_inputs.reshape(slot_shape + (model_width,)))
-    gate_grad_home = exchange(gate_grad.reshape(slot_shape))
+    grad_home = exchange(after(grad_inputs.reshape(slot_shape + (model_width,)), cot_seq))
+    gate_grad_home = lax.all_gather(
+        gate_grad.reshape(expert_count, seq_dev * capacity), "expert", axis=0
+    )
+    gate_grad_home = lax.dynamic_index_in_dim(gate_grad_home, my_index, 1, keepdims=False)
     result = (
         jnp.einsum("rf,df->rd", activated_low, w_second, preferred_element_type=wide) * gate_rows
     ).astype(low)
-    coming_back = exchange(result.reshape(slot_shape + (model_width,)))
+    coming_back = exchange(after(result.reshape(slot_shape + (model_width,)), grad_home))
     grad_flat = (gate_rows * cot_rows.astype(wide)).astype(low)
     grad_first_w = jnp.einsum("rd,rf->df", received, grad_before, preferred_element_type=wide)
     grad_second_w = jnp.einsum("rd,rf->df", grad_flat, activated_low, preferred_element_type=wide)
@@ -358,17 +539,19 @@
         frozen * (jnp.arange(frozen.shape[0], dtype=jnp.int32) == my_index).astype(jnp.int32)
     )
     trainable = (1 - flag_value).astype(wide)
-    expert_stack = jnp.stack([grad_first_w, grad_second_w]) * trainable
-    expert_grad = lax.psum_scatter(
-        expert_stack.astype(low), "dp", scatter_dimension=2, tiled=True
-    ).astype(wide)
-
-    gate_grad_flat = jnp.swapaxes(gate_grad_home, 0, 1).reshape(seq_dev, 1, slots)
+    expert_stack = jnp.stack(
+        [(grad_first_w * trainable).astype(low), (grad_second_w * trainable).astype(low)]
+    )
+    expert_sum = lax.psum_scatter(expert_stack, "dp", scatter_dimension=2, tiled=True)
+
+    gate_grad_flat = jnp.swapaxes(
+        gate_grad_home.reshape(expert_count, seq_dev, capacity), 0, 1
+    ).reshape(seq_dev, 1, slots)
     grad_gate = jnp.stack(
-        [jnp.sum(jnp.where(hits[k], gate_grad_flat, 0.0), axis=-1) for k in range(TOP)], axis=-1
-    )
-    grad_chosen = gates * (grad_gate - jnp.sum(gates * grad_gate, axis=-1, keepdims=True))
-    grad_logits = jnp.sum(onehot_four * grad_chosen[..., None], axis=2).reshape(
+        [jnp.sum(jnp.where(hits[k], gate_grad_flat, 0.0), axis=-1) for k in range(TOP)], axis=1
+    )
+    grad_chosen = gates * (grad_gate - jnp.sum(gates * grad_gate, axis=1, keepdims=True))
+    grad_logits = jnp.sum(onehot_four * grad_chosen[..., None], axis=1).reshape(
         row_count, expert_total
     )
     router_local = jnp.dot(low_two_wide.T, grad_logits, precision=precise)
@@ -410,37 +593,24 @@
     grad_w_project = jnp.einsum("rd,re->de", low_one, grad_projected, preferred_element_type=wide)
     grad_norms = jnp.stack([gain_one, gain_two, bias_one, bias_two])
     block_width = attend_master.shape[2]
-    grad_full = jnp.concatenate([grad_w_project, grad_w_output], axis=1).astype(low)
     slot_range = jnp.arange(expert_count, dtype=jnp.int32)
     which_block = jnp.sum(
         slot_range[None, :] * (owner_list[None, :] == slot_range[:, None]).astype(jnp.int32), axis=1
     )
-    small = jnp.concatenate([router_local.reshape(-1), grad_norms.reshape(-1)])
-    small_rows = small.shape[0] // block_width
-    padded_rows = -(-small_rows // (16 * dp_count)) * 16 * dp_count
-    small = jnp.pad(
-        small.astype(low).reshape(small_rows, block_width), ((0, padded_rows - small_rows), (0, 0))
-    )
-    to_owner = jnp.stack(
-        [
-            jnp.concatenate(
-                [
-                    lax.dynamic_slice_in_dim(
-                        grad_full, which_block[s] * block_width, block_width, 1
-                    ),
-                    small,
-                ]
-            )
-            for s in range(expert_count)
-        ]
-    )
-    my_rows = lax.psum_scatter(to_owner, "dp", scatter_dimension=1, tiled=True)
-    my_rows = jnp.sum(exchange(my_rows).astype(wide), axis=0)
+    small_width = expert_total + 4
+    small = jnp.concatenate([router_local, grad_norms.T], axis=1).astype(low)
+    small = jnp.pad(small, ((0, 0), (0, 128 - small_width)))
+    grad_full = jnp.concatenate(
+        [grad_w_project.astype(low), grad_w_output.astype(low), small], axis=1
+    )
+    my_rows = sum_dp(grad_full)
+    my_rows = exchange(deal(which_block, my_rows, block_width, expert_count))
+    my_rows = jnp.sum(my_rows.astype(wide), axis=0)
     summed = lax.all_gather(my_rows, "dp", axis=0, tiled=True)
-    block_grad = summed[:model_width]
-    small_sum = summed[model_width : model_width + small_rows].reshape(-1)
-    router_grad = small_sum[: router.size].reshape(router.shape)
-    norm_grad = small_sum[router.size :].reshape(grad_norms.shape)
+    block_grad = summed[:, :block_width]
+    small_sum = summed[:, block_width : block_width + small_width]
+    router_grad = small_sum[:, :expert_total]
+    norm_grad = small_sum[:, expert_total:].T
 
     left_basis = attend_left[0].astype(low)
     right_basis = attend_right[0].astype(low)
@@ -451,24 +621,14 @@
     stepped = dot_low(dot_low(left_basis, direction, ROW_COL), right_basis, ROW_ROW)
     attend_master_new = attend_master[0] - matrix_rate * stepped
 
-    basis = expert_basis[0].astype(low)
-    is_frozen = flag_value > 0
-    news = []
-    for i in range(2):
-        rotated_one = dot_low(basis, expert_grad[i], COL_COL)
-        first_new, second_new, move = adam_move(rotated_one, expert_first[0, i], expert_second[0, i])
-        master_new = expert_master[0, i] - matrix_rate * dot_low(basis, move, ROW_COL)
-        master_new = jnp.where(is_frozen, expert_master[0, i], master_new)
-        news.append(
-            (
-                master_new,
-                jnp.where(is_frozen, expert_first[0, i], first_new),
-                jnp.where(is_frozen, expert_second[0, i], second_new),
-                average_keep * expert_average[0, i] + (1.0 - average_keep) * master_new,
-            )
-        )
-    expert_master_new, expert_first_new, expert_second_new, expert_average_new = (
-        jnp.stack(pair) for pair in zip(*news)
+    expert_grad, expert_master_new, expert_first_new, expert_second_new, expert_average_new = refresh(
+        flag_value.astype(jnp.int32).reshape(1),
+        expert_basis[0].astype(low),
+        expert_sum,
+        expert_master,
+        expert_first,
+        expert_second,
+        expert_average,
     )
 
     router_first_new, router_second_new, router_step = adam_move(
@@ -493,11 +653,11 @@
         attend_master_new[None],
         attend_first_new[None],
         attend_second_new[None],
-        expert_grad[None],
-        expert_master_new[None],
-        expert_first_new[None],
-        expert_second_new[None],
-        expert_average_new[None],
+        expert_grad,
+        expert_master_new,
+        expert_first_new,
+        expert_second_new,
+        expert_average_new,
     )
 
 

time: 971 us -> 886 us (0.912)
  blocking collectives: 116 us -> 295 us
  waiting for transfers between devices: 271 us -> 124 us
  Pallas kernels: 60.2 us -> 139 us
  matrix products: 210 us -> 135 us
  other arithmetic: 123 us -> 54.9 us
  local copies, waits for them, and re-layouts: 120 us -> 75.4 us
    all_gather x0 -> x3, blocking collectives: none -> 253 us  [the longest x1 106 us: on_device(): all_codes = lax.all_gather(home_code, 'expert', axis=0)]
    all_to_all x5 -> x4, waiting for transfers between devices: 201 us -> 61.4 us  [exchange(): lax.all_to_all(value, 'expert', split_axis=0, concat_axis=0, tiled=True)]
    pallas_call x0 -> x3, Pallas kernels: none -> 78.4 us  [the longest x1 51.4 us: expert_stage(): pl.pallas_call(expert_kernel, grid=(rows // TILE,), out_shape=(jax.ShapeD...]
    all_to_all x2 -> x1, blocking collectives: 103 us -> 42.3 us  [exchange(): lax.all_to_all(value, 'expert', split_axis=0, concat_axis=0, tiled=True)]
    dot_general x3 -> x1, matrix products: 72.1 us -> 18.6 us  [on_device(): jnp.dot(cot_rows, w_second, preferred_element_type=wide).astype(low)]
    unnamed x178 -> x110, local copies, waits for them, and re-layouts: 70.7 us -> 20.8 us
    convert_element_type x3 -> x2, other arithmetic: 45.6 us -> 5.97 us  [the longest x1 3 us: sum_dp(): half = (kept.astype(wide) + got.astype(wide)).astype(low)]
    all_to_all x4, waiting for transfers between devices: 70.2 us -> 35.1 us  [swap(): lax.all_to_all(value, 'expert', split_axis=0, concat_axis=0, tiled=True,...]
  transfers between devices with their start and end apart: 12 -> 12, of which waited for: 8 -> 4; matrix products, arithmetic and copies ran while one was open for 26% -> 25% of each run, Pallas kernels for 2% -> 16%
where the time goes in v2:
time: 886 us; the launch traced here: 880 us
  blocking collectives  295 us (33%)
  Pallas kernels  139 us (16%)
  matrix products  135 us (15%)
  waiting for transfers between devices  124 us (14%)
  local copies, waits for them, and re-layouts  75.4 us (9%)
  other arithmetic  54.9 us (6%)
  starting transfers between devices  42.2 us (5%)
  between operations  15.7 us (2%)
    all_gather x1, blocking collectives, on_device(): all_codes = lax.all_gather(home_code, 'expert', axis=0)  106 us
    all_gather x1, blocking collectives, on_device(): gate_rows = lax.all_gather(gate_slots, 'expert', axis=0)  88.4 us
    all_to_all x4, waiting for transfers between devices, exchange(): lax.all_to_all(value, 'expert', split_axis=0, concat_axis=0, tiled=True)  61.4 us
    all_gather x1, blocking collectives, on_device(): lax.all_gather(gate_grad.reshape(expert_count, seq_dev * capacity), 'expe...  58.1 us
    pallas_call x1, Pallas kernels, expert_stage(): pl.pallas_call(expert_kernel, grid=(rows // TILE,), out_shape=(jax.ShapeD...  51.4 us
    all_to_all x1, blocking collectives, exchange(): lax.all_to_all(value, 'expert', split_axis=0, concat_axis=0, tiled=True)  42.3 us
    pallas_call x1, Pallas kernels, attend_back(): pl.pallas_call(functools.partial(attend_back_kernel, whole), grid=(pairs,...  38.2 us
    all_to_all x4, waiting for transfers between devices, swap(): lax.all_to_all(value, 'expert', split_axis=0, concat_axis=0, tiled=True,...  35.1 us
  transfers between devices with their start and end apart: 12, of which 4 were waited for; matrix products, arithmetic and copies ran while one was open for 25% of the time, Pallas kernels for 16%

profile of v2, /device:TPU:0, one launch (start us, length us, event | category | flops | bytes accessed | tf_op | source)
XLA Modules:
  0.0 880.5 jit_solution(3747607476277177052)
XLA Ops:
  7.2 7.6 all-to-all-start
  20.0 4.6 convert_bitcast_fusion
  24.5 27.4 %all-to-all-done = bf16[8,128,768]{2,1,0:T(8,128)(2,1)} async-done(((bf16[8,128,768]{2,1,0:T(8,128)(2,1)}), bf16[8,128,768]{2,1,0:T(8,128)(2,1)}, u32[]{:S(2)}, u32[]{:S(2)}) %all-to-all-start) | async-done | bytes 1572896 | tf_op jit(solution)/shard_map/all_to_all | solution.py:416
  51.9 4.3 copy.350
  56.2 4.5 all-to-all-start.1
  61.4 106.3 %all-gather = s32[64,2,128]{2,1,0:T(2,128)S(1)} all-gather(s32[8,2,128]{2,1,0:T(2,128)} %copy.348), channel_id=2, replica_groups=mesh['dp'=4,'expert'=8] {'expert'}, dimensions={0}, use_global_device_ids=true | all-gather | bytes 73728 | tf_op jit(solution)/shard_map/all_gather | solution.py:450
  171.6 1.7 convert_reduce_fusion
  173.4 2.0 fusion.17
  175.9 2.0 fusion.24
  178.0 5.5 convolution_convert_fusion.1.q_ref.k_ref.v_ref
  183.5 22.1 %attend.1 = (bf16[1024,768]{1,0:T(8,128)(2,1)}, f32[1024,768]{1,0:T(8,128)}) custom-call(s32[1]{0:T(128)} %bitcast.1.start_ref, bf16[1024,2304]{1,0:T(8,128)(2,1)} %convolution_convert_fusion.1.q_ref.k_ref.v_ref, bf16[1024,2304]{1,0:T(8,128)(2,1)} %convolution_convert_fusion.1.q_ref.k_ref.v_ref, bf16[1024,2304]{1,0:T(8,128)(2,1)} %convolution_convert_fusion.1.q_ref.k_ref.v_ref), custom_call_target="tpu_custom_call" | custom-call | flops 1610612736 | bytes 9437184 | tf_op jit(solution)/shard_map/attend/pallas_call | solution.py:164
  205.5 3.8 fusion.101
  212.3 2.3 convert_bitcast_fusion.1
  214.6 4.3 copy.351
  218.9 4.9 all-to-all-start.2
  225.2 5.0 slice_bitcast_fusion.w_ref
  238.0 88.4 %all_gather.17 = f32[8,8,320]{2,1,0:T(8,128)S(1)} all-gather(f32[1,8,320]{2,1,0:T(8,128)} %all_gather_reshape.6), channel_id=1, replica_groups=mesh['dp'=4,'expert'=8] {'expert'}, dimensions={0}, use_global_device_ids=true | all-gather | bytes 92160 | tf_op jit(solution)/shard_map/all_gather | solution.py:516
  327.1 2.9 reshape.273.gate_ref
  330.0 4.3 copy.352
  334.3 4.3 all-to-all-start.3
  338.6 18.6 %convolution_convert_fusion.u_ref = bf16[2560,3072]{1,0:T(8,128)(2,1)} fusion(bf16[2560,768]{1,0:T(8,128)(2,1)} %bitcast.216, bf16[1,2,768,3072]{3,2,1,0:T(8,128)(2,1)} %param.33), kind=kOutput, calls=%fused_computation.1 | convolution fusion | flops 12087459840 | bytes 24379392 | tf_op jit(solution)/shard_map/dot_general | solution.py:521
  357.2 51.4 %expert_stage.1 = (bf16[2560,3072]{1,0:T(8,128)(2,1)}, bf16[2560,3072]{1,0:T(8,128)(2,1)}, bf16[2560,768]{1,0:T(8,128)(2,1)}, f32[2560,1]{1,0:T(8,128)}) custom-call(bf16[2560,768]{1,0:T(8,128)(2,1)} %bitcast.22.x_ref, bf16[2560,3072]{1,0:T(8,128)(2,1)} %convolution_convert_fusion.u_ref, f32[2560,1]{1,0:T(8,128)} %reshape.273.gate_ref, ...), custom_call_target="tpu_custom_call" | custom-call | flops 24159191040 | bytes 47185920 | tf_op jit(solution)/shard_map/expert_stage/pallas_call | solution.py:250
  408.6 6.1 all-to-all-start.4
  417.5 17.9 %multiply_convert_fusion.3 = bf16[2560,768]{1,0:T(8,128)(2,1)} fusion(bf16[2560,3072]{1,0:T(8,128)(2,1)} %get-tuple-element.41, bf16[1,2,768,3072]{3,2,1,0:T(8,128)(2,1)} %param.33, f32[2560]{0:T(1024)} %mul.282), kind=kOutput, calls=%fused_computation.8 | convolution fusion | flops 12083527680 | bytes 24391680 | tf_op jit(solution)/shard_map/rf,df->rd/dot_general | solution.py:532
  435.4 61.4 %all-to-all-done.4 = bf16[8,8,40,768]{3,2,1,0:T(8,128)(2,1)} async-done(((bf16[8,8,40,768]{3,2,1,0:T(8,128)(2,1)}), bf16[8,8,40,768]{3,2,1,0:T(8,128)(2,1)}, u32[]{:S(2)}, u32[]{:S(2)}) %all-to-all-start.4) | async-done | bytes 3932192 | tf_op jit(solution)/shard_map/all_to_all | solution.py:437
  496.9 4.5 all-to-all-start.5
  501.4 18.6 %fusion.6 = bf16[1,768,3072]{2,1,0:T(8,128)(2,1)} fusion(f32[]{:T(128)S(6)} %convert_element_type.193, bf16[2560,768]{1,0:T(8,128)(2,1)} %bitcast.22.x_ref, bf16[2560,3072]{1,0:T(8,128)(2,1)} %get-tuple-element.51), kind=kOutput, calls=%fused_computation.17 | convolution fusion | flops 12084314112 | bytes 24379396 | tf_op jit(solution)/shard_map/rd,rf->df/dot_general | solution.py:536
  520.0 18.0 %fusion.7 = bf16[1,768,3072]{2,1,0:T(8,128)(2,1)} fusion(f32[]{:T(128)S(6)} %convert_element_type.193, bf16[2560,3072]{1,0:T(8,128)(2,1)} %get-tuple-element.41, bf16[2560,768]{1,0:T(8,128)(2,1)S(1)} %bitcast.217, f32[2560]{0:T(1024)S(1)} %copy-done.47), kind=kOutput, calls=%fused_computation.18 | convolution fusion | flops 12090212352 | bytes 24389636 | tf_op jit(solution)/shard_map/rd,rf->df/dot_general | solution.py:537
  538.0 8.3 pad_maximum_fusion
  546.3 2.3 reduce.8
  550.1 58.1 %all_gather.18 = f32[8,8,320]{2,1,0:T(8,128)S(1)} all-gather(f32[1,8,320]{2,1,0:T(8,128)} %all_gather_reshape.7), channel_id=1, replica_groups=mesh['dp'=4,'expert'=8] {'expert'}, dimensions={0}, use_global_device_ids=true | all-gather | bytes 92160 | tf_op jit(solution)/shard_map/all_gather | solution.py:527
  616.3 2.7 convolution_convert_fusion.7
  619.0 3.4 fusion.10
  622.5 5.5 multiply_reduce_fusion
  630.4 3.4 fusion.12
  634.4 3.8 convert_add_fusion.1
  638.2 2.6 convolution_convert_fusion.3.g_ref
  640.8 38.2 %attend_back.1 = (bf16[1024,768]{1,0:T(8,128)(2,1)}, bf16[1024,768]{1,0:T(8,128)(2,1)}, bf16[1024,768]{1,0:T(8,128)(2,1)}) custom-call(s32[1]{0:T(128)} %bitcast.1.start_ref, bf16[1024,2304]{1,0:T(8,128)(2,1)} %convolution_convert_fusion.1.q_ref.k_ref.v_ref, bf16[1024,2304]{1,0:T(8,128)(2,1)} %convolution_convert_fusion.1.q_ref.k_ref.v_ref, ...), custom_call_target="tpu_custom_call" | custom-call | flops 4026531840 | bytes 15728640 | tf_op jit(solution)/shard_map/attend_back/pallas_call | solution.py:189
  681.6 8.2 fusion.30
  692.1 4.0 convolution_convert_fusion.4
  696.4 4.3 convolution_convert_fusion.2
  701.1 2.3 copy-done.6
  705.7 4.8 fusion.29
  710.4 4.3 all-to-all-start.7
  714.8 3.0 fusion.3
  722.5 27.6 %collective-permute-done.1 = bf16[192,3200]{1,0:T(8,128)(2,1)} collective-permute-done((bf16[192,3200]{1,0:T(8,128)(2,1)}, bf16[192,3200]{1,0:T(8,128)(2,1)}, u32[]{:S(2)}, u32[]{:S(2)}) %collective-permute-start.1) | collective-permute-done | bytes 1228832 | tf_op jit(solution)/shard_map/ppermute | solution.py:433
  750.1 3.0 fusion.31.block_ref.small_ref
  753.0 6.1 deal.1
  759.1 42.3 %all_to_all.45 = bf16[8,192,512]{2,1,0:T(8,128)(2,1)} all-to-all(bf16[8,192,512]{2,1,0:T(8,128)(2,1)} %deal.1), channel_id=1, replica_groups=mesh['dp'=4,'expert'=8] {'expert'}, dimensions={0} | all-to-all | bytes 3145728 | tf_op jit(solution)/shard_map/all_to_all | solution.py:437
  801.4 4.3 all-to-all-start.6
  805.8 2.4 convert_reduce_fusion.1
  808.2 2.7 copy.367
  810.9 2.4 copy.368.basis_ref
  813.3 20.9 %refresh.1 = (f32[1,2,768,768]{3,2,1,0:T(8,128)}, f32[1,2,768,768]{3,2,1,0:T(8,128)}, f32[1,2,768,768]{3,2,1,0:T(8,128)}, f32[1,2,768,768]{3,2,1,0:T(8,128)}, f32[1,2,768,768]{3,2,1,0:T(8,128)}) custom-call(s32[1]{0:T(128)} %bitcast.63.flag_ref, bf16[768,768]{1,0:T(8,128)(2,1)} %copy.368.basis_ref, bf16[768,768]{1,0:T(8,128)(2,1)} %bitcast.212, ...), custom_call_target="tpu_custom_call" | custom-call | flops 3623878656 | bytes 44826624 | tf_op jit(solution)/shard_map/refresh/pallas_call | solution.py:309
  834.2 7.7 all-to-all-done.6
  841.8 4.7 fusion.38
  846.5 3.7 fusion.65
  850.2 6.2 fusion.34
  856.4 1.8 slice.72
  858.2 1.7 copy.378
  859.9 1.9 slice.71
  865.8 2.4 slice_bitcast_fusion.1
  868.1 2.7 copy.393
  870.8 2.7 copy.394
  (184 shorter events, 54.3 us)
Async XLA Ops:
  7.2 170.8 %copy-start = (bf16[768,2304]{1,0:T(8,128)(2,1)S(1)}, bf16[768,2304]{1,0:T(8,128)(2,1)}, u32[]{:S(2)}) copy-start(bf16[768,2304]{1,0:T(8,128)(2,1)} %param.28) | copy-start | bytes 10616836
  7.2 7.6 copy-start.41
  7.2 44.7 %all-to-all-start = ((bf16[8,128,768]{2,1,0:T(8,128)(2,1)}), bf16[8,128,768]{2,1,0:T(8,128)(2,1)}, u32[]{:S(2)}, u32[]{:S(2)}) async-start(bf16[8,128,768]{2,1,0:T(8,128)(2,1)} %param.26), calls=%async_computation | async-start | bytes 3145728 | tf_op jit(solution)/shard_map/all_to_all | solution.py:416
  19.2 151.4 %copy-start.21 = (s32[8,40]{1,0:T(8,128)}, s32[8,40]{1,0:T(8,128)S(1)}, u32[]{:S(2)}) copy-start(s32[8,40]{1,0:T(8,128)S(1)} %multiply_add_fusion.2) | copy-start | bytes 3844
  56.2 158.4 %all-to-all-start.1 = ((bf16[8,8,40,768]{3,2,1,0:T(8,128)(2,1)}), bf16[8,8,40,768]{3,2,1,0:T(8,128)(2,1)}, u32[]{:S(2)}, u32[]{:S(2)}) async-start(bf16[8,8,40,768]{3,2,1,0:T(8,128)(2,1)} %copy.350), calls=%async_computation.1 | async-start | bytes 7864320 | tf_op jit(solution)/shard_map/all_to_all | solution.py:437
  169.2 1.4 copy-start.24
  170.6 4.7 copy-start.34
  173.3 2.0 copy-start.36
  175.3 0.6 copy-start.38
  178.0 5.5 copy-start.11
  209.3 1.6 copy-start.1
  209.3 0.7 copy-start.26
  209.3 0.7 copy-start.42
  209.9 1.2 copy-start.15
  209.9 2.4 copy-start.29
  210.9 1.3 copy-start.4
  218.9 115.4 %all-to-all-start.2 = ((bf16[8,8,40,768]{3,2,1,0:T(8,128)(2,1)}), bf16[8,8,40,768]{3,2,1,0:T(8,128)(2,1)}, u32[]{:S(2)}, u32[]{:S(2)}) async-start(bf16[8,8,40,768]{3,2,1,0:T(8,128)(2,1)} %copy.351), calls=%async_computation.2 | async-start | bytes 7864320 | tf_op jit(solution)/shard_map/all_to_all | solution.py:437
  225.2 5.0 copy-start.5
  225.2 5.0 copy-start.19
  225.2 6.3 copy-start.25
  231.6 0.6 copy-start.23
  231.6 102.7 %copy-start.40 = (f32[8,128]{1,0:T(8,128)}, f32[8,128]{1,0:T(8,128)S(1)}, u32[]{:S(2)}) copy-start(f32[8,128]{1,0:T(8,128)S(1)} %get-tuple-element.224) | copy-start | bytes 12292
  334.3 74.3 %all-to-all-start.3 = ((bf16[8,128,768]{2,1,0:T(8,128)(2,1)}), bf16[8,128,768]{2,1,0:T(8,128)(2,1)}, u32[]{:S(2)}, u32[]{:S(2)}) async-start(bf16[8,128,768]{2,1,0:T(8,128)(2,1)} %param.27), calls=%async_computation.3 | async-start | bytes 3145728 | tf_op jit(solution)/shard_map/all_to_all | solution.py:416
  408.6 6.1 copy-start.49
  408.6 88.2 %all-to-all-start.4 = ((bf16[8,8,40,768]{3,2,1,0:T(8,128)(2,1)}), bf16[8,8,40,768]{3,2,1,0:T(8,128)(2,1)}, u32[]{:S(2)}, u32[]{:S(2)}) async-start(bf16[8,8,40,768]{3,2,1,0:T(8,128)(2,1)} %bitcast.218), calls=%async_computation.4 | async-start | bytes 7864320 | tf_op jit(solution)/shard_map/all_to_all | solution.py:437
  496.9 133.5 %all-to-all-start.5 = ((bf16[8,8,40,768]{3,2,1,0:T(8,128)(2,1)}), bf16[8,8,40,768]{3,2,1,0:T(8,128)(2,1)}, u32[]{:S(2)}, u32[]{:S(2)}) async-start(bf16[8,8,40,768]{3,2,1,0:T(8,128)(2,1)} %bitcast.215), calls=%async_computation.5 | async-start | bytes 7864320 | tf_op jit(solution)/shard_map/all_to_all | solution.py:437
  501.4 311.9 %reduce-scatter.2.cloned.1.call-start = ((), (), s32[]{:S(2)}) async-start(), calls=%async_computation.11 | async-start | bytes 11796480 | tf_op jit(solution)/shard_map/reduce_scatter | solution.py:545
  501.4 18.6 %copy-start.10 = (bf16[1,8,8,40,768]{4,3,2,1,0:T(8,128)(2,1)S(1)}, bf16[1,8,8,40,768]{4,3,2,1,0:T(8,128)(2,1)}, u32[]{:S(2)}) copy-start(bf16[1,8,8,40,768]{4,3,2,1,0:T(8,128)(2,1)} %copy.352) | copy-start | bytes 11796484
  501.4 18.6 %copy-start.47 = (f32[2560]{0:T(1024)S(1)}, f32[2560]{0:T(1024)}, u32[]{:S(2)}) copy-start(f32[2560]{0:T(1024)} %mul.282) | copy-start | bytes 30724
  546.3 72.7 %copy-start.22 = (s32[8,40]{1,0:T(8,128)S(1)}, s32[8,40]{1,0:T(8,128)}, u32[]{:S(2)}) copy-start(s32[8,40]{1,0:T(8,128)} %copy-done.21) | copy-start | bytes 3844
  619.0 3.4 copy-start.2
  619.0 3.4 copy-start.20
  619.0 3.4 copy-start.27
  619.0 3.4 copy-start.30
  630.4 3.4 copy-start.3
  630.4 4.0 copy-start.8
  630.4 4.0 copy-start.28
  630.4 4.0 copy-start.31
  630.4 4.0 copy-start.43
  630.4 4.0 copy-start.44
  634.4 3.8 copy-start.48
  638.2 2.6 copy-start.7
  678.9 1.9 copy-start.14
  678.9 2.4 copy-start.13
  680.8 0.8 copy-start.35
  680.8 0.8 copy-start.37
  680.8 0.8 copy-start.39
  681.6 8.2 copy-start.17
  681.6 8.2 copy-start.45
  681.6 8.2 copy-start.46
  681.6 8.3 copy-start.32
  692.1 4.0 copy-start.12
  692.1 4.2 copy-start.18
  696.4 4.3 copy-start.16
  701.1 2.3 copy-start.6
  705.0 9.8 %collective-permute-start = (bf16[2,192,3200]{2,1,0:T(8,128)(2,1)}, bf16[2,192,3200]{2,1,0:T(8,128)(2,1)}, u32[]{:S(2)}, u32[]{:S(2)}) collective-permute-start(bf16[2,192,3200]{2,1,0:T(8,128)(2,1)} %dynamic-slice_bitcast_fusion), channel_id=1, source_target_pairs={{0,8},{8,0},{16,24},{24,16},{1,9},{9,1},{17,25},{25,17},{2,10},{10... | collective-permute-start | bytes 7372808 | tf_op jit(solution)/shard_map/ppermute | solution.py:427
  710.4 48.7 %all-to-all-start.7 = ((bf16[8,128,768]{2,1,0:T(8,128)(2,1)}), bf16[8,128,768]{2,1,0:T(8,128)(2,1)}, u32[]{:S(2)}, u32[]{:S(2)}) async-start(bf16[8,128,768]{2,1,0:T(8,128)(2,1)} %bitcast.214), calls=%async_computation.7 | async-start | bytes 3145728 | tf_op jit(solution)/shard_map/all_to_all | solution.py:416
  714.7 7.1 copy-start.50
  717.8 1.4 copy-start.9
  720.3 29.7 %collective-permute-start.1 = (bf16[192,3200]{1,0:T(8,128)(2,1)}, bf16[192,3200]{1,0:T(8,128)(2,1)}, u32[]{:S(2)}, u32[]{:S(2)}) collective-permute-start(bf16[192,3200]{1,0:T(8,128)(2,1)} %dynamic-slice_bitcast_fusion.1), channel_id=1, source_target_pairs={{0,16},{8,24},{16,0},{24,8},{1,17},{9,25},{17,1},{25,9},{2,18},{10... | collective-permute-start | bytes 3686408 | tf_op jit(solution)/shard_map/ppermute | solution.py:433
  801.4 40.4 %all-to-all-start.6 = ((bf16[8,128,768]{2,1,0:T(8,128)(2,1)}), bf16[8,128,768]{2,1,0:T(8,128)(2,1)}, u32[]{:S(2)}, u32[]{:S(2)}) async-start(bf16[8,128,768]{2,1,0:T(8,128)(2,1)} %bitcast.213), calls=%async_computation.6 | async-start | bytes 3145728 | tf_op jit(solution)/shard_map/all_to_all | solution.py:416
  805.7 36.1 %all-gather.3.cloned.1.call-start = ((), (), s32[]{:S(2)}) async-start(), calls=%async_computation.10 | async-start | bytes 1966080 | tf_op jit(solution)/shard_map/all_gather | solution.py:609
  863.0 10.5 %copy-start.33 = (f32[768,4]{0,1:T(4,128)}, f32[768,4]{0,1:T(4,128)S(1)}, u32[]{:S(2)}) copy-start(f32[768,4]{0,1:T(4,128)S(1)} %copy.377) | copy-start | bytes 36868
Sparse Core Ops, SparseCore 0:
  546.4 79.0 reduce-scatter.1
  808.7 20.9 all-gather.2
